TPU v7x, 32 devices: a 4x4x1 block of a 4x4x8 slice. The times are simulated.
32 devices in a mesh: batch: 1 (over z), row: 4 (over y), col: 8 (over x, core).
Axes of the slice: x: 4, y: 4, z: 1, core: 2. Of those that a mesh axis runs over, the one named last changes fastest.
The devices are a block of a 4x4x8 slice.
Arguments:
- lower_tri: bfloat16 [6144, 6144], P(('batch', 'row'), 'col')
- right_side: bfloat16 [6144, 32768], P(('batch', 'row'), 'col')
- grad_out: bfloat16 [6144, 32768], P(('batch', 'row'), 'col')
Outputs:
- output 1: bfloat16 [6144, 32768], P(('batch', 'row'), 'col')
- output 2: bfloat16 [6144, 6144], P(('batch', 'row'), 'col')
All inputs are finite; a program needn't handle non-finite values.
Results may differ from a plain program's by a relative error of at most 0.001.
Values are sent between devices in bfloat16 or wider.
A program may use at most 768 MiB of HBM per device.

v0:
```python
import jax
import jax.numpy as jnp
from jax import lax
from jax.sharding import PartitionSpec as P

BLOCK_SIZE = 256


def solution(mesh):
    mesh_rows = mesh.shape["row"]
    mesh_cols = mesh.shape["col"]
    group_size = max(mesh_rows, mesh_cols)
    row_step = group_size // mesh_rows
    col_step = group_size // mesh_cols
    block_spec = P(("batch", "row"), "col")

    def per_device(lower_tri, right_side, grad_out):
        rows_here, cols_here = lower_tri.shape
        num_cols = right_side.shape[1]
        num_steps = rows_here // (row_step * BLOCK_SIZE)
        right_pieces = []
        lower_pieces = []
        for step_idx in range(num_steps):
            first_row = step_idx * row_step * BLOCK_SIZE
            left_rows = rows_here - first_row
            grad_rows = grad_out[first_row:]
            lower_panel = lower_tri[first_row:, step_idx * col_step * BLOCK_SIZE:(step_idx + 1) * col_step * BLOCK_SIZE]
            gathered = lax.all_gather(lower_panel.reshape(left_rows, col_step, BLOCK_SIZE), "col", axis=2)
            right_part = jnp.einsum("rbqe,rf->bqef", gathered, grad_rows, preferred_element_type=jnp.float32)
            right_mine = lax.psum_scatter(right_part.reshape(row_step, mesh_rows * BLOCK_SIZE, num_cols), "row", scatter_dimension=1, tiled=True)
            right_pieces.append(right_mine.reshape(row_step * BLOCK_SIZE, num_cols).astype(jnp.bfloat16))
            side_block = right_side[first_row:first_row + row_step * BLOCK_SIZE].reshape(row_step, BLOCK_SIZE, num_cols)
            side_rows = lax.all_gather(side_block, "row", axis=1).reshape(col_step, mesh_cols, BLOCK_SIZE, num_cols)
            lower_part = jnp.einsum("rf,bqef->rbqe", grad_rows, side_rows, preferred_element_type=jnp.float32)
            lower_mine = lax.psum_scatter(lower_part.reshape(left_rows, col_step, mesh_cols * BLOCK_SIZE), "col", scatter_dimension=2, tiled=True)
            lower_piece = lower_mine.reshape(left_rows, col_step * BLOCK_SIZE).astype(jnp.bfloat16)
            lower_pieces.append(jnp.pad(lower_piece, ((first_row, 0), (0, 0))))
        grad_right = jnp.concatenate(right_pieces, axis=0)
        grad_lower = jnp.concatenate(lower_pieces, axis=1)
        row_pos = jnp.arange(rows_here)[:, None]
        col_pos = jnp.arange(cols_here)[None, :]
        row_global = (row_pos // BLOCK_SIZE * mesh_rows + lax.axis_index("row")) * BLOCK_SIZE + row_pos % BLOCK_SIZE
        col_global = (col_pos // BLOCK_SIZE * mesh_cols + lax.axis_index("col")) * BLOCK_SIZE + col_pos % BLOCK_SIZE
        grad_lower = jnp.where(row_global >= col_global, grad_lower, 0.0).astype(jnp.bfloat16)
        return grad_right, grad_lower

    return jax.shard_map(per_device, mesh=mesh, in_specs=(block_spec, block_spec, block_spec), out_specs=(block_spec, block_spec), check_vma=False)
```

profile of v0, /device:TPU:97, one launch (start us, length us, event | category | flops | bytes accessed | tf_op | source)
XLA Modules:
  0.0 1627.6 jit_solution(6735920215824656914)
XLA Ops:
  7.2 0.1 all-gather.14.cloned.1.call-start
  7.2 9.0 fusion.45
  16.3 0.1 all-gather.12.cloned.1.call-start
  16.4 0.7 all-gather.12.cloned.1.call-update
  17.2 0.1 all-gather.10.cloned.1.call-start
  17.2 0.7 all-gather.10.cloned.1.call-update
  17.9 0.1 all-gather.20.cloned.1.call-start
  18.0 0.7 slice.27
  18.8 0.1 all-gather.20.cloned.1.call-update
  18.8 0.1 all-gather.18.cloned.1.call-start
  18.9 0.8 slice.25
  19.8 0.1 all-gather.16.cloned.1.call-start
  19.8 0.9 slice.24
  20.8 0.1 reduce-scatter.17.cloned.1.call-start
  20.9 151.6 %all-gather.14.cloned.1.call-done = bf16[2,4,256,4096]{3,2,1,0:T(8,128)(2,1)} async-done(((bf16[2,1,256,4096]{3,2,1,0:T(8,128)(2,1)}), bf16[2,4,256,4096]{3,2,1,0:T(8,128)(2,1)}) %all-gather.14.cloned.1.call-update) | async-done | bytes 16777232 | tf_op jit(solution)/shard_map/all_gather | solution.py:33
  172.5 15.1 fusion.18
  187.6 0.1 reduce-scatter.15.cloned.1.call-start
  187.7 139.7 %all-gather.12.cloned.1.call-done = bf16[2,4,256,4096]{3,2,1,0:T(8,128)(2,1)} async-done(((bf16[2,1,256,4096]{3,2,1,0:T(8,128)(2,1)}), bf16[2,4,256,4096]{3,2,1,0:T(8,128)(2,1)}) %all-gather.12.cloned.1.call-update) | async-done | bytes 16777232 | tf_op jit(solution)/shard_map/all_gather | solution.py:33
  327.4 24.2 %fusion.10 = f32[1024,1,2048]{2,0,1:T(8,128)} fusion(bf16[2048,4096]{1,0:T(8,128)(2,1)} %bitcast.62, bf16[1536,4096]{1,0:T(8,128)(2,1)} %param.5), kind=kOutput, calls=%fused_computation.16 | convolution fusion | flops 17179869184 | bytes 33554432 | tf_op jit(solution)/shard_map/rf,bqef->rbqe/dot_general | solution.py:34
  351.7 0.2 reduce-scatter.13.cloned.1.call-start
  351.9 131.0 %all-gather.10.cloned.1.call-done = bf16[2,4,256,4096]{3,2,1,0:T(8,128)(2,1)} async-done(((bf16[2,1,256,4096]{3,2,1,0:T(8,128)(2,1)}), bf16[2,4,256,4096]{3,2,1,0:T(8,128)(2,1)}) %all-gather.10.cloned.1.call-update) | async-done | bytes 16777232 | tf_op jit(solution)/shard_map/all_gather | solution.py:33
  482.9 34.5 %convolution_bitcast_fusion = f32[1536,1,2048]{2,0,1:T(8,128)} fusion(bf16[1536,4096]{1,0:T(8,128)(2,1)} %param.5, bf16[2048,4096]{1,0:T(8,128)(2,1)} %bitcast.61), kind=kOutput, calls=%fused_computation.3 | convolution fusion | flops 25769803776 | bytes 41943040 | tf_op jit(solution)/shard_map/rf,bqef->rbqe/dot_general | solution.py:34
  517.5 0.1 reduce-scatter.11.cloned.1.call-start
  517.6 2.9 copy.13
  520.5 16.7 %fusion.13 = f32[2,1024,4096]{2,1,0:T(8,128)} fusion(bf16[2,1024,512]{2,1,0:T(8,128)(2,1)S(1)} %bitcast.60, bf16[1536,4096]{1,0:T(8,128)(2,1)} %param.5), kind=kOutput, calls=%fused_computation.17 | convolution fusion | flops 8589934592 | bytes 39845888 | tf_op jit(solution)/shard_map/rbqe,rf->bqef/dot_general | solution.py:29
  537.3 0.1 reduce-scatter.9.cloned.1.call-start
  537.4 7.2 all-gather.18.cloned.1.call-done
  544.6 6.4 copy.12
  550.9 25.0 %fusion.2 = f32[2,1024,4096]{2,1,0:T(8,128)} fusion(bf16[2,1024,1024]{2,1,0:T(8,128)(2,1)} %bitcast.59, bf16[1536,4096]{1,0:T(8,128)(2,1)} %param.5), kind=kOutput, calls=%fused_computation.4 | convolution fusion | flops 17179869184 | bytes 46137344 | tf_op jit(solution)/shard_map/rbqe,rf->bqef/dot_general | solution.py:29
  576.0 0.3 reduce-scatter.7.cloned.1.call-start
  576.3 12.4 all-gather.16.cloned.1.call-done
  588.7 8.7 copy.11
  597.4 33.8 %fusion = f32[2,1024,4096]{2,1,0:T(8,128)} fusion(bf16[2,1024,1536]{2,1,0:T(8,128)(2,1)} %bitcast.58, bf16[1536,4096]{1,0:T(8,128)(2,1)} %param.5), kind=kOutput, calls=%fused_computation.1 | convolution fusion | flops 25769803776 | bytes 52428800 | tf_op jit(solution)/shard_map/rbqe,rf->bqef/dot_general | solution.py:29
  631.3 1.1 convert_bitcast_fusion.2
  632.4 45.3 %reduce-scatter.15.cloned.1.call-done = f32[1024,1,256]{2,0,1:T(8,128)} async-done(((f32[1024,1,2048]{2,0,1:T(8,128)}), f32[1024,1,256]{2,0,1:T(8,128)}) %reduce-scatter.15.cloned.1.call-update) | async-done | bytes 1048592 | tf_op jit(solution)/shard_map/reduce_scatter | solution.py:35
  677.7 1.3 convert_bitcast_fusion.1
  679.0 71.2 %reduce-scatter.13.cloned.1.call-done = f32[1536,1,256]{2,0,1:T(8,128)} async-done(((f32[1536,1,2048]{2,0,1:T(8,128)}), f32[1536,1,256]{2,0,1:T(8,128)}) %reduce-scatter.13.cloned.1.call-update) | async-done | bytes 1572880 | tf_op jit(solution)/shard_map/reduce_scatter | solution.py:35
  750.2 1.5 convert_bitcast_fusion
  751.7 2.9 compare_select_fusion
  754.5 278.1 %reduce-scatter.11.cloned.1.call-done = f32[2,256,4096]{2,1,0:T(8,128)} async-done(((f32[2,1024,4096]{2,1,0:T(8,128)}), f32[2,256,4096]{2,1,0:T(8,128)}) %reduce-scatter.11.cloned.1.call-update) | async-done | bytes 8388624 | tf_op jit(solution)/shard_map/reduce_scatter | solution.py:30
  1032.6 6.0 convert_element_type.46
  1038.6 276.3 %reduce-scatter.9.cloned.1.call-done = f32[2,256,4096]{2,1,0:T(8,128)} async-done(((f32[2,1024,4096]{2,1,0:T(8,128)}), f32[2,256,4096]{2,1,0:T(8,128)}) %reduce-scatter.9.cloned.1.call-update) | async-done | bytes 8388624 | tf_op jit(solution)/shard_map/reduce_scatter | solution.py:30
  1315.0 6.0 convert_element_type.44
  1320.9 276.2 %reduce-scatter.7.cloned.1.call-done = f32[2,256,4096]{2,1,0:T(8,128)} async-done(((f32[2,1024,4096]{2,1,0:T(8,128)}), f32[2,256,4096]{2,1,0:T(8,128)}) %reduce-scatter.7.cloned.1.call-update) | async-done | bytes 8388624 | tf_op jit(solution)/shard_map/reduce_scatter | solution.py:30
  1597.2 4.1 convert_element_type.42
  1601.3 0.4 copy-done
  1601.8 1.3 copy-done.1
  1603.0 17.7 %pad_maximum_fusion = bf16[1536,4096]{1,0:T(8,128)(2,1)} fusion(bf16[512,4096]{1,0:T(8,128)(2,1)S(1)} %bitcast.52, bf16[512,4096]{1,0:T(8,128)(2,1)S(1)} %bitcast.53, bf16[512,4096]{1,0:T(8,128)(2,1)S(1)} %bitcast.54), kind=kLoop, calls=%fused_computation | loop fusion | flops 37748736 | bytes 25165824 | tf_op jit(solution)/shard_map/concatenate | solution.py:38
  (17 shorter events, 0.6 us)
Async XLA Ops:
  7.2 165.4 %all-gather.14.cloned.1.call-start = ((), (), s32[]{:S(2)}) async-start(), calls=%async_computation.13 | async-start | bytes 20971520 | tf_op jit(solution)/shard_map/all_gather | solution.py:33
  16.3 1.7 copy-start.2
  16.3 311.1 %all-gather.12.cloned.1.call-start = ((), (), s32[]{:S(2)}) async-start(), calls=%async_computation.11 | async-start | bytes 20971520 | tf_op jit(solution)/shard_map/all_gather | solution.py:33
  17.2 465.8 %all-gather.10.cloned.1.call-start = ((), (), s32[]{:S(2)}) async-start(), calls=%async_computation.9 | async-start | bytes 20971520 | tf_op jit(solution)/shard_map/all_gather | solution.py:33
  17.9 499.7 %all-gather.20.cloned.1.call-start = ((), (), s32[]{:S(2)}) async-start(), calls=%async_computation.17 | async-start | bytes 2359296 | tf_op jit(solution)/shard_map/all_gather | solution.py:28
  18.8 525.7 %all-gather.18.cloned.1.call-start = ((), (), s32[]{:S(2)}) async-start(), calls=%async_computation.16 | async-start | bytes 4718592 | tf_op jit(solution)/shard_map/all_gather | solution.py:28
  19.8 568.9 %all-gather.16.cloned.1.call-start = ((), (), s32[]{:S(2)}) async-start(), calls=%async_computation.15 | async-start | bytes 7077888 | tf_op jit(solution)/shard_map/all_gather | solution.py:28
  20.8 610.5 %reduce-scatter.17.cloned.1.call-start = ((), (), s32[]{:S(2)}) async-start(), calls=%async_computation.14 | async-start | bytes 4718592 | tf_op jit(solution)/shard_map/reduce_scatter | solution.py:35
  187.6 490.0 %reduce-scatter.15.cloned.1.call-start = ((), (), s32[]{:S(2)}) async-start(), calls=%async_computation.12 | async-start | bytes 9437184 | tf_op jit(solution)/shard_map/reduce_scatter | solution.py:35
  351.7 398.5 %reduce-scatter.13.cloned.1.call-start = ((), (), s32[]{:S(2)}) async-start(), calls=%async_computation.10 | async-start | bytes 14155776 | tf_op jit(solution)/shard_map/reduce_scatter | solution.py:35
  517.5 515.1 %reduce-scatter.11.cloned.1.call-start = ((), (), s32[]{:S(2)}) async-start(), calls=%async_computation.8 | async-start | bytes 41943040 | tf_op jit(solution)/shard_map/reduce_scatter | solution.py:30
  537.3 777.7 %reduce-scatter.9.cloned.1.call-start = ((), (), s32[]{:S(2)}) async-start(), calls=%async_computation.7 | async-start | bytes 41943040 | tf_op jit(solution)/shard_map/reduce_scatter | solution.py:30
  576.0 1021.1 %reduce-scatter.7.cloned.1.call-start = ((), (), s32[]{:S(2)}) async-start(), calls=%async_computation.6 | async-start | bytes 41943040 | tf_op jit(solution)/shard_map/reduce_scatter | solution.py:30
  1597.2 4.6 copy-start
  1597.2 5.9 copy-start.1
Sparse Core Ops, SparseCore 0:
  16.5 156.0 all-gather.13
  174.1 153.2 all-gather.11
  329.6 153.3 all-gather.9
  484.4 25.4 all-gather.19
  511.3 33.2 all-gather.17
  546.6 42.0 all-gather.15
  591.0 32.9 reduce-scatter.16
  626.4 51.2 reduce-scatter.14
  680.6 69.5 reduce-scatter.12
  752.4 280.1 reduce-scatter.10
  1035.0 279.9 reduce-scatter.8
  1317.2 279.9 reduce-scatter.6
where the time goes:
time: 1630 us
  waiting for transfers between devices  1390 us (85%)
  matrix products  149 us (9%)
  other arithmetic  40.6 us (2%)
  local copies, waits for them, and re-layouts  31.1 us (2%)
    reduce_scatter x3, waiting for transfers between devices, per_device(): lax.psum_scatter(right_part.reshape(row_step, mesh_rows * BLOCK_SIZE, num...  831 us
    all_gather x3, waiting for transfers between devices, per_device(): lax.all_gather(side_block, 'row', axis=1)  422 us
    reduce_scatter x3, waiting for transfers between devices, per_device(): lax.psum_scatter(lower_part.reshape(left_rows, col_step, mesh_cols * BLOC...  117 us
    dot_general x3, matrix products, per_device(): jnp.einsum('rbqe,rf->bqef', gathered, grad_rows, preferred_element_type=j...  75.6 us
    dot_general x3, matrix products, per_device(): jnp.einsum('rf,bqef->rbqe', grad_rows, side_rows, preferred_element_type=...  73.8 us
  transfers between devices with their start and end apart: 12, of which 10 were waited for; matrix products, arithmetic and copies ran while one was open for 12% of the time, Pallas kernels for 0%

commit v1 on v0

v1 whole, which is shorter than its diff:
```python
import jax
import jax.numpy as jnp
from jax import lax
from jax.sharding import PartitionSpec as P


BLOCK_SIZE = 256


def solution(mesh):
    mesh_rows = mesh.shape["row"]
    mesh_cols = mesh.shape["col"]
    halves = mesh_cols // mesh_rows
    block_spec = P(("batch", "row"), "col")
    up = [(row, (row + 1) % mesh_rows) for row in range(mesh_rows)]
    down = [(row, (row - 1) % mesh_rows) for row in range(mesh_rows)]

    spread = []
    collect = [[] for _ in range(halves)]
    for row in range(mesh_rows):
        for col in range(mesh_cols):
            home, half = col % mesh_rows, col // mesh_rows
            spread.append((row * mesh_cols + col, home * mesh_cols + half * mesh_rows + (row - home) % mesh_rows))
            rel, part = col // halves, col % halves
            for turn in range(halves):
                owner = (row + rel) % mesh_rows * mesh_cols + row + mesh_rows * ((part + turn) % halves)
                collect[turn].append((row * mesh_cols + col, owner))

    def shards(lower_tri, right_side, grad_out):
        rows_here, cols_here = lower_tri.shape
        num_groups = rows_here // BLOCK_SIZE
        num_supers = num_groups // halves
        my_col = lax.axis_index("col")
        my_half = my_col // mesh_rows
        my_part = my_col % halves

        own = [grad_out[group * BLOCK_SIZE:(group + 1) * BLOCK_SIZE] for group in range(num_groups)]
        near = {}
        far = {}
        panels = {
            sup: lower_tri[sup * halves * BLOCK_SIZE:(sup + 1) * halves * BLOCK_SIZE, :(sup + 1) * BLOCK_SIZE]
            for sup in range(num_supers)
        }
        totals = {}
        sends = {}
        received = {}
        state = {"out": jnp.zeros(right_side.shape, jnp.bfloat16)}

        def send_own(group):
            near[group] = (lax.ppermute(own[group], "row", up), lax.ppermute(own[group], "row", down))

        def spread_panel(sup):
            panel = lax.ppermute(panels[sup], ("row", "col"), spread)
            panels[sup] = lax.all_gather(panel, "col", axis=0)

        def forward(group):
            waits = list(near[group])
            later = group - 2
            if later >= 0:
                waits.append(own[later])
            if group + 2 in totals:
                waits.append(totals[group + 2])
            waits = list(lax.optimization_barrier(tuple(waits)))
            prev_block, next_block = near[group] = (waits.pop(0), waits.pop(0))
            far[group] = (
                lax.ppermute(prev_block[:BLOCK_SIZE // 2], "row", up),
                lax.ppermute(next_block[BLOCK_SIZE // 2:], "row", down),
            )
            if later >= 0:
                own[later] = waits.pop(0)
                send_own(later)
            if group + 2 in totals:
                totals[group + 2] = waits.pop(0)

        def collect_lower(group):
            received[group] = [lax.ppermute(send, ("row", "col"), collect[turn]) for turn, send in enumerate(sends[group])]

        def compute(group):
            width = (group + 1) * BLOCK_SIZE
            sup = group // halves
            waits = [own[group], near[group][1], *far[group], near[group][0], panels[sup]]
            if group > 0:
                waits += near[group - 1]
            if group + 1 in totals:
                waits.append(totals[group + 1])
            if group + 2 in sends:
                waits += sends[group + 2]
            waits = list(lax.optimization_barrier(tuple(waits)))
            blocks, panels[sup] = waits[:5], waits[5]
            waits = waits[6:]
            if group > 0:
                near[group - 1] = (waits.pop(0), waits.pop(0))
            if group + 1 in totals:
                totals[group + 1] = waits.pop(0)
            if group + 2 in sends:
                sends[group + 2] = waits
                collect_lower(group + 2)

            panel = panels[sup].reshape(halves, mesh_rows, halves, BLOCK_SIZE, sup + 1, BLOCK_SIZE)[:, :, group % halves]
            panel = panel.transpose(1, 2, 3, 0, 4).reshape(mesh_rows * BLOCK_SIZE, (sup + 1) * halves * BLOCK_SIZE)
            grad_rows = jnp.concatenate(blocks, axis=0)
            lower_part = lax.dot_general(
                grad_rows, right_side[:width], (((1,), (1,)), ((), ())), preferred_element_type=jnp.float32
            )
            grad_rows, lower_part = lax.optimization_barrier((grad_rows, lower_part))
            lower_mine = lax.psum_scatter(lower_part, "col", scatter_dimension=0, tiled=True)
            lower_mine = lower_mine.astype(jnp.bfloat16)
            total = lax.dot_general(
                panel[:, :width], grad_rows, (((0,), (0,)), ((), ())), preferred_element_type=jnp.float32
            )
            if group + 1 in totals:
                total = totals[group + 1][:width] + total
            totals[group] = total
            done = total[group * BLOCK_SIZE:].astype(jnp.bfloat16)
            state["out"] = lax.dynamic_update_slice(state["out"], done, (group * BLOCK_SIZE, 0))

            lower_mine = jnp.pad(lower_mine, ((0, 0), (0, (sup + 1) * halves * BLOCK_SIZE - width)))
            lower_mine = lower_mine.reshape(-1, sup + 1, halves, BLOCK_SIZE)
            pieces = [lower_mine[:, :, half].reshape(-1, (sup + 1) * BLOCK_SIZE) for half in range(halves)]
            sends[group] = []
            for turn in range(halves):
                send = pieces[turn]
                for part in range(1, halves):
                    send = jnp.where(my_part == part, pieces[(part + turn) % halves], send)
                sends[group].append(send)

        for sup in reversed(range(num_supers)):
            spread_panel(sup)
        send_own(num_groups - 1)
        send_own(num_groups - 2)
        forward(num_groups - 1)
        for group in reversed(range(num_groups)):
            if group > 0:
                forward(group - 1)
            compute(group)
        collect_lower(1)
        collect_lower(0)

        lower_rows = []
        for group in range(num_groups):
            for part in range(halves):
                piece = received[group][0]
                for turn in range(1, halves):
                    piece = jnp.where((my_half - part) % halves == turn, received[group][turn], piece)
                lower_rows.append(jnp.pad(piece, ((0, 0), (0, cols_here - piece.shape[1]))))
        grad_lower = jnp.concatenate(lower_rows, axis=0)
        row_pos = jnp.arange(rows_here)[:, None]
        col_pos = jnp.arange(cols_here)[None, :]
        row_global = (row_pos // BLOCK_SIZE * mesh_rows + lax.axis_index("row")) * BLOCK_SIZE + row_pos % BLOCK_SIZE
        col_global = (col_pos // BLOCK_SIZE * mesh_cols + my_col) * BLOCK_SIZE + col_pos % BLOCK_SIZE
        grad_lower = jnp.where(row_global >= col_global, grad_lower, 0.0).astype(jnp.bfloat16)
        return state["out"], grad_lower

    return jax.shard_map(shards, mesh=mesh, in_specs=(block_spec, block_spec, block_spec), out_specs=(block_spec, block_spec), check_vma=False)
```

time: 1630 us -> 743 us (0.46)
  waiting for transfers between devices: 1390 us -> 158 us
  local copies, waits for them, and re-layouts: 31.1 us -> 266 us
  starting transfers between devices: 1.17 us -> 114 us
  other arithmetic: 40.6 us -> 14.2 us
  matrix products: 149 us -> 167 us
    reduce_scatter x6, waiting for transfers between devices: 947 us -> 0.48 us  [compute(): lax.psum_scatter(lower_part, 'col', scatter_dimension=0, tiled=True)]
    all_gather x6 -> x3, waiting for transfers between devices: 442 us -> 18.3 us  [spread_panel(): panels[sup] = lax.all_gather(panel, 'col', axis=0)]
    ppermute x0 -> x39, waiting for transfers between devices: none -> 138 us  [the longest x6 82.2 us: send_own(): lax.ppermute(own[group], 'row', up)]
    ppermute x0 -> x39, starting transfers between devices: none -> 114 us  [the longest x12 47 us: collect_lower(): lax.ppermute(send, ('row', 'col'), collect[turn])]
    slice x4 -> x24, local copies, waits for them, and re-layouts: 11.5 us -> 76.2 us  [the longest x3 39.1 us: compute(): panels[sup]]
    unnamed x6 -> x106, local copies, waits for them, and re-layouts: 1.7 us -> 64.3 us
    reshape x1 -> x13, local copies, waits for them, and re-layouts: 8.67 us -> 49.4 us  [the longest x4 33.2 us: compute(): panels[sup]]
    transpose x0 -> x10, local copies, waits for them, and re-layouts: none -> 29 us  [compute(): panel.transpose(1, 2, 3, 0, 4)]
  transfers between devices with their start and end apart: 12 -> 48, of which waited for: 10 -> 16; matrix products, arithmetic and copies ran while one was open for 12% -> 50% of each run, Pallas kernels for 0% -> 0%
where the time goes in v1:
time: 743 us; the launch traced here: 735 us
  local copies, waits for them, and re-layouts  266 us (36%)
  matrix products  167 us (22%)
  waiting for transfers between devices  158 us (21%)
  starting transfers between devices  114 us (15%)
  between operations  15 us (2%)
  other arithmetic  14.2 us (2%)
    dot_general x6, matrix products, compute(): lax.dot_general(panel[:, :width], grad_rows, (((0,), (0,)), ((), ())), pr...  96.4 us
    ppermute x6, waiting for transfers between devices, send_own(): lax.ppermute(own[group], 'row', up)  82.2 us
    dot_general x6, matrix products, compute(): lax.dot_general(grad_rows, right_side[:width], (((1,), (1,)), ((), ())),...  70.9 us
    unnamed x106, local copies, waits for them, and re-layouts  64.3 us
    ppermute x12, starting transfers between devices, collect_lower(): lax.ppermute(send, ('row', 'col'), collect[turn])  47 us
    slice x3, local copies, waits for them, and re-layouts, compute(): panels[sup]  39.1 us
    reshape x4, local copies, waits for them, and re-layouts, compute(): panels[sup]  33.2 us
    ppermute x6, starting transfers between devices, send_own(): lax.ppermute(own[group], 'row', down)  31.5 us
  transfers between devices with their start and end apart: 48, of which 16 were waited for; matrix products, arithmetic and copies ran while one was open for 50% of the time, Pallas kernels for 0%

profile of v1, /device:TPU:97, one launch (start us, length us, event | category | flops | bytes accessed | tf_op | source)
XLA Modules:
  0.0 735.1 jit_solution(14768658362694496641)
XLA Ops:
  8.4 5.7 collective-permute-start.4
  14.1 9.1 %collective-permute-done.4 = bf16[512,768]{1,0:T(8,128)(2,1)S(1)} collective-permute-done((bf16[512,768]{1,0:T(8,128)(2,1)S(1)}, bf16[512,768]{1,0:T(8,128)(2,1)S(1)}, u32[]{:S(2)}, u32[]{:S(2)}) %collective-permute-start.4) | collective-permute-done | bytes 786464 | tf_op jit(solution)/shard_map/ppermute | solution.py:53
  24.2 8.4 %fusion.49 = (bf16[256,4096]{1,0:T(8,128)(2,1)}, bf16[256,4096]{1,0:T(8,128)(2,1)}, bf16[256,4096]{1,0:T(8,128)(2,1)S(1)}, bf16[256,4096]{1,0:T(8,128)(2,1)}, bf...) fusion(bf16[1536,4096]{1,0:T(8,128)(2,1)} %param.5), kind=kLoop, calls=%fused_computation.128 | loop fusion | bytes 25165824 | tf_op jit(solution)/shard_map/slice | solution.py:37
  33.8 10.9 %collective-permute-start.1 = (bf16[256,4096]{1,0:T(8,128)(2,1)S(1)}, bf16[256,4096]{1,0:T(8,128)(2,1)S(1)}, u32[]{:S(2)}, u32[]{:S(2)}) collective-permute-start(bf16[256,4096]{1,0:T(8,128)(2,1)S(1)} %get-tuple-element.98), channel_id=1, source_target_pairs={{0,24},{8,0},{16,8},{24,16},{1,25},{9,1},{17,9},{25,17},{2,26},{10... | collective-permute-start | bytes 6291464 | tf_op jit(solution)/shard_map/ppermute | solution.py:50
  47.3 42.4 %collective-permute-done = bf16[256,4096]{1,0:T(8,128)(2,1)S(1)} collective-permute-done((bf16[256,4096]{1,0:T(8,128)(2,1)S(1)}, bf16[256,4096]{1,0:T(8,128)(2,1)S(1)}, u32[]{:S(2)}, u32[]{:S(2)}) %collective-permute-start) | collective-permute-done | bytes 2097184 | tf_op jit(solution)/shard_map/ppermute | solution.py:50
  94.9 39.8 %collective-permute-done.5 = bf16[256,4096]{1,0:T(8,128)(2,1)S(1)} collective-permute-done((bf16[256,4096]{1,0:T(8,128)(2,1)S(1)}, bf16[256,4096]{1,0:T(8,128)(2,1)S(1)}, u32[]{:S(2)}, u32[]{:S(2)}) %collective-permute-start.5) | collective-permute-done | bytes 2097184 | tf_op jit(solution)/shard_map/ppermute | solution.py:50
  140.3 16.8 %collective-permute-done.2 = bf16[128,4096]{1,0:T(8,128)(2,1)S(1)} collective-permute-done((bf16[128,4096]{1,0:T(8,128)(2,1)S(1)}, bf16[128,4096]{1,0:T(8,128)(2,1)S(1)}, u32[]{:S(2)}, u32[]{:S(2)}) %collective-permute-start.2) | collective-permute-done | bytes 1048608 | tf_op jit(solution)/shard_map/ppermute | solution.py:66
  159.1 8.6 %copy.26 = bf16[8,512,768]{1,2,0:T(8,128)(2,1)} copy(bf16[8,512,768]{2,1,0:T(8,128)(2,1)} %bitcast.74) | data formatting | bytes 12582912 | tf_op jit(solution)/shard_map/optimization_barrier | solution.py:88
  167.7 9.7 %reshape.200 = bf16[2,4,2,256,3,256]{3,2,5,4,1,0:T(2,128)(2,1)} reshape(bf16[8,512,768]{1,2,0:T(8,128)(2,1)} %copy.26) | data formatting | bytes 12582912 | tf_op jit(solution)/shard_map/reshape | solution.py:99
  177.4 8.9 %slice.233 = bf16[2,4,1,256,3,256]{3,2,5,4,1,0:T(2,128)(2,1)} slice(bf16[2,4,2,256,3,256]{3,2,5,4,1,0:T(2,128)(2,1)} %reshape.200), slice={[0:2], [0:4], [1:2], [0:256], [0:3], [0:256]} | slice | bytes 6291456 | tf_op jit(solution)/shard_map/slice | solution.py:99
  186.4 15.1 %copy.27 = bf16[2,4,1,256,3,256]{5,3,4,2,1,0:T(8,128)(2,1)} copy(bf16[2,4,1,256,3,256]{3,2,5,4,1,0:T(2,128)(2,1)} %slice.233) | data formatting | bytes 6291456 | tf_op jit(solution)/shard_map/slice | solution.py:99
  201.4 5.1 copy.28
  218.4 17.4 %fusion.54 = f32[1024,1536]{1,0:T(8,128)} fusion(bf16[1024,4096]{1,0:T(8,128)(2,1)S(1)} %constant_dynamic-update-slice_fusion, bf16[1536,4096]{1,0:T(8,128)(2,1)} %param.4), kind=kOutput, calls=%fused_computation.133 | convolution fusion | flops 12884901888 | bytes 27262976 | tf_op jit(solution)/shard_map/dot_general | solution.py:102
  235.8 20.5 %fusion.55 = f32[1536,4096]{1,0:T(8,128)} fusion(bf16[1024,1536]{1,0:T(8,128)(2,1)S(1)} %copy-done.16, bf16[1024,4096]{1,0:T(8,128)(2,1)} %copy-done.21), kind=kOutput, calls=%fused_computation.134 | convolution fusion | flops 12884901888 | bytes 36700160 | tf_op jit(solution)/shard_map/dot_general | solution.py:108
  263.0 16.7 %fusion = f32[1024,1280]{1,0:T(8,128)} fusion(bf16[1024,4096]{1,0:T(8,128)(2,1)S(1)} %constant_dynamic-update-slice_fusion.5, bf16[1536,4096]{1,0:T(8,128)(2,1)} %param.4), kind=kOutput, calls=%fused_computation.3 | convolution fusion | flops 10737418240 | bytes 24117248 | tf_op jit(solution)/shard_map/dot_general | solution.py:102
  281.8 6.4 collective-permute-start.13
  288.2 10.7 %collective-permute-done.13 = bf16[512,512]{1,0:T(8,128)(2,1)S(1)} collective-permute-done((bf16[512,512]{1,0:T(8,128)(2,1)S(1)}, bf16[512,512]{1,0:T(8,128)(2,1)S(1)}, u32[]{:S(2)}, u32[]{:S(2)}) %collective-permute-start.13) | collective-permute-done | bytes 524320 | tf_op jit(solution)/shard_map/ppermute | solution.py:53
  300.2 8.4 %collective-permute-start.15 = (bf16[256,4096]{1,0:T(8,128)(2,1)}, bf16[256,4096]{1,0:T(8,128)(2,1)}, u32[]{:S(2)}, u32[]{:S(2)}) collective-permute-start(bf16[256,4096]{1,0:T(8,128)(2,1)} %get-tuple-element.142), channel_id=1, source_target_pairs={{0,24},{8,0},{16,8},{24,16},{1,25},{9,1},{17,9},{25,17},{2,26},{10... | collective-permute-start | bytes 6291464 | tf_op jit(solution)/shard_map/ppermute | solution.py:50
  313.3 8.7 %copy.29 = bf16[8,512,768]{1,2,0:T(8,128)(2,1)} copy(bf16[8,512,768]{2,1,0:T(8,128)(2,1)} %bitcast.75) | data formatting | bytes 12582912 | tf_op jit(solution)/shard_map/optimization_barrier | solution.py:88
  322.0 9.7 %reshape.202 = bf16[2,4,2,256,3,256]{3,2,5,4,1,0:T(2,128)(2,1)} reshape(bf16[8,512,768]{1,2,0:T(8,128)(2,1)} %copy.29) | data formatting | bytes 12582912 | tf_op jit(solution)/shard_map/reshape | solution.py:99
  331.8 15.1 %copy.30 = bf16[2,4,1,256,3,256]{5,3,4,2,1,0:T(8,128)(2,1)} copy(bf16[2,4,1,256,3,256]{3,2,5,4,1,0:T(2,128)(2,1)} %bitcast.76) | data formatting | bytes 6291456 | tf_op jit(solution)/shard_map/slice | solution.py:99
  346.9 5.2 copy.31
  358.2 22.8 %slice_add_fusion = f32[1280,4096]{1,0:T(8,128)} fusion(f32[1536,4096]{1,0:T(8,128)} %fusion.55, bf16[1024,4096]{1,0:T(8,128)(2,1)} %copy-done.22, bf16[1024,1536]{1,0:T(8,128)(2,1)} %reshape.203), kind=kOutput, calls=%fused_computation | convolution fusion | flops 10742661120 | bytes 52953088 | tf_op jit(solution)/shard_map/dot_general | solution.py:108
  402.2 6.9 reshape.205
  412.2 4.6 copy.34
  416.7 4.4 reshape.206
  432.3 12.6 %fusion.2 = f32[1024,1024]{1,0:T(8,128)} fusion(bf16[1024,4096]{1,0:T(8,128)(2,1)S(1)} %constant_dynamic-update-slice_fusion.10, bf16[1536,4096]{1,0:T(8,128)(2,1)} %param.4), kind=kOutput, calls=%fused_computation.6 | convolution fusion | flops 8589934592 | bytes 20971520 | tf_op jit(solution)/shard_map/dot_general | solution.py:102
  445.0 18.8 %slice_add_fusion.1 = f32[1024,4096]{1,0:T(8,128)} fusion(f32[1280,4096]{1,0:T(8,128)} %slice_add_fusion, bf16[1024,1024]{1,0:T(8,128)(2,1)} %reshape.206, bf16[1024,4096]{1,0:T(8,128)(2,1)} %copy-done.2), kind=kOutput, calls=%fused_computation.1 | convolution fusion | flops 8594128896 | bytes 44040192 | tf_op jit(solution)/shard_map/dot_general | solution.py:108
  473.7 11.1 %fusion.4 = f32[1024,768]{1,0:T(8,128)} fusion(bf16[1024,4096]{1,0:T(8,128)(2,1)S(1)} %constant_dynamic-update-slice_fusion.15, bf16[1536,4096]{1,0:T(8,128)(2,1)} %param.4), kind=kOutput, calls=%fused_computation.8 | convolution fusion | flops 6442450944 | bytes 17825792 | tf_op jit(solution)/shard_map/dot_general | solution.py:102
  489.6 5.4 collective-permute-done.22
  498.5 6.3 collective-permute-start.24
  504.8 6.6 dynamic_update_slice.18
  516.1 6.9 reshape.208
  526.0 4.6 copy.37
  530.6 4.5 reshape.209
  537.7 14.3 %slice_add_fusion.2 = f32[768,4096]{1,0:T(8,128)} fusion(f32[1024,4096]{1,0:T(8,128)} %slice_add_fusion.1, bf16[1024,4096]{1,0:T(8,128)(2,1)} %copy-done.3, bf16[1024,1024]{1,0:T(8,128)(2,1)} %reshape.209), kind=kOutput, calls=%fused_computation.2 | convolution fusion | flops 6445596672 | bytes 35127296 | tf_op jit(solution)/shard_map/dot_general | solution.py:108
  564.5 16.1 %all-gather.11.cloned.1.call-done = bf16[4096,256]{1,0:T(8,128)(2,1)} async-done(((bf16[512,256]{1,0:T(8,128)(2,1)}), bf16[4096,256]{1,0:T(8,128)(2,1)}) %all-gather.11.cloned.1.call-update) | async-done | bytes 2097168 | tf_op jit(solution)/shard_map/all_gather | solution.py:54
  594.3 8.0 %fusion.6 = f32[1024,512]{1,0:T(8,128)} fusion(bf16[1024,4096]{1,0:T(8,128)(2,1)S(1)} %constant_dynamic-update-slice_fusion.20, bf16[1536,4096]{1,0:T(8,128)(2,1)} %param.4), kind=kOutput, calls=%fused_computation.17 | convolution fusion | flops 4294967296 | bytes 14680064 | tf_op jit(solution)/shard_map/dot_general | solution.py:102
  602.3 11.7 %slice_add_fusion.3 = f32[512,4096]{1,0:T(8,128)} fusion(f32[768,4096]{1,0:T(8,128)} %slice_add_fusion.2, bf16[1024,512]{1,0:T(8,128)(2,1)S(1)} %bitcast.81, bf16[1024,4096]{1,0:T(8,128)(2,1)} %copy-done.1), kind=kOutput, calls=%fused_computation.5 | convolution fusion | flops 4297064448 | bytes 26214400 | tf_op jit(solution)/shard_map/dot_general | solution.py:108
  623.7 5.0 fusion.17
  634.9 6.6 collective-permute-start.36
  652.7 4.7 collective-permute-start.31
  657.5 4.9 collective-permute-start.32
  666.2 8.3 %fusion.12 = bf16[1536,4096]{1,0:T(8,128)(2,1)} fusion(bf16[1536,4096]{1,0:T(8,128)(2,1)} %fusion.16, f32[512,4096]{1,0:T(8,128)} %slice_add_fusion.3, bf16[1024,4096]{1,0:T(8,128)(2,1)} %copy-done, bf16[1024,512]{1,0:T(8,128)(2,1)S(1)} %bitcast.84), kind=kOutput, calls=%fused_computation.21 | convolution fusion | flops 2149580800 | bytes 15204352 | tf_op jit(solution)/shard_map/dot_general | solution.py:108
  690.5 6.2 collective-permute-done.28
  699.0 4.9 collective-permute-start.29
  704.0 4.8 collective-permute-start.30
  709.5 7.0 collective-permute-start.38
  (260 shorter events, 202.5 us)
Async XLA Ops:
  7.2 151.9 %all-gather.7.cloned.1.call-start = ((), (), s32[]{:S(2)}) async-start(), calls=%async_computation.12 | async-start | bytes 7077888 | tf_op jit(solution)/shard_map/all_gather | solution.py:54
  8.4 14.8 %collective-permute-start.4 = (bf16[512,768]{1,0:T(8,128)(2,1)S(1)}, bf16[512,768]{1,0:T(8,128)(2,1)S(1)}, u32[]{:S(2)}, u32[]{:S(2)}) collective-permute-start(bf16[512,768]{1,0:T(8,128)(2,1)S(1)} %slice.180), channel_id=1, source_target_pairs={{0,0},{1,11},{2,18},{3,25},{4,4},{5,15},{6,22},{7,29},{8,1},{9,8},... | collective-permute-start | bytes 2359304 | tf_op jit(solution)/shard_map/ppermute | solution.py:53
  24.1 364.7 %reduce-scatter.9.cloned.1.call-start = ((), (), s32[]{:S(2)}) async-start(), calls=%async_computation.7 | async-start | bytes 5898240 | tf_op jit(solution)/shard_map/reduce_scatter | solution.py:106
  32.6 57.1 %collective-permute-start = (bf16[256,4096]{1,0:T(8,128)(2,1)S(1)}, bf16[256,4096]{1,0:T(8,128)(2,1)S(1)}, u32[]{:S(2)}, u32[]{:S(2)}) collective-permute-start(bf16[256,4096]{1,0:T(8,128)(2,1)S(1)} %get-tuple-element.98), channel_id=1, source_target_pairs={{0,8},{8,16},{16,24},{24,0},{1,9},{9,17},{17,25},{25,1},{2,10},{10... | collective-permute-start | bytes 6291464 | tf_op jit(solution)/shard_map/ppermute | solution.py:50
  33.8 57.8 %collective-permute-start.1 = (bf16[256,4096]{1,0:T(8,128)(2,1)S(1)}, bf16[256,4096]{1,0:T(8,128)(2,1)S(1)}, u32[]{:S(2)}, u32[]{:S(2)}) collective-permute-start(bf16[256,4096]{1,0:T(8,128)(2,1)S(1)} %get-tuple-element.98), channel_id=1, source_target_pairs={{0,24},{8,0},{16,8},{24,16},{1,25},{9,1},{17,9},{25,17},{2,26},{10... | collective-permute-start | bytes 6291464 | tf_op jit(solution)/shard_map/ppermute | solution.py:50
  44.6 90.0 %collective-permute-start.5 = (bf16[256,4096]{1,0:T(8,128)(2,1)S(1)}, bf16[256,4096]{1,0:T(8,128)(2,1)S(1)}, u32[]{:S(2)}, u32[]{:S(2)}) collective-permute-start(bf16[256,4096]{1,0:T(8,128)(2,1)S(1)} %get-tuple-element.112), channel_id=1, source_target_pairs={{0,8},{8,16},{16,24},{24,0},{1,9},{9,17},{17,25},{25,1},{2,10},{10... | collective-permute-start | bytes 6291464 | tf_op jit(solution)/shard_map/ppermute | solution.py:50
  45.4 91.2 %collective-permute-start.6 = (bf16[256,4096]{1,0:T(8,128)(2,1)S(1)}, bf16[256,4096]{1,0:T(8,128)(2,1)S(1)}, u32[]{:S(2)}, u32[]{:S(2)}) collective-permute-start(bf16[256,4096]{1,0:T(8,128)(2,1)S(1)} %get-tuple-element.112), channel_id=1, source_target_pairs={{0,24},{8,0},{16,8},{24,16},{1,25},{9,1},{17,9},{25,17},{2,26},{10... | collective-permute-start | bytes 6291464 | tf_op jit(solution)/shard_map/ppermute | solution.py:50
  91.7 65.4 %collective-permute-start.2 = (bf16[128,4096]{1,0:T(8,128)(2,1)S(1)}, bf16[128,4096]{1,0:T(8,128)(2,1)S(1)}, u32[]{:S(2)}, u32[]{:S(2)}) collective-permute-start(bf16[128,4096]{1,0:T(8,128)(2,1)S(1)} %slice.178), channel_id=1, source_target_pairs={{0,8},{8,16},{16,24},{24,0},{1,9},{9,17},{17,25},{25,1},{2,10},{10... | collective-permute-start | bytes 3145736 | tf_op jit(solution)/shard_map/ppermute | solution.py:66
  93.3 65.8 %collective-permute-start.3 = (bf16[128,4096]{1,0:T(8,128)(2,1)S(1)}, bf16[128,4096]{1,0:T(8,128)(2,1)}, u32[]{:S(2)}, u32[]{:S(2)}) collective-permute-start(bf16[128,4096]{1,0:T(8,128)(2,1)S(1)} %slice.179), channel_id=1, source_target_pairs={{0,24},{8,0},{16,8},{24,16},{1,25},{9,1},{17,9},{25,17},{2,26},{10... | collective-permute-start | bytes 3145736 | tf_op jit(solution)/shard_map/ppermute | solution.py:67
  94.7 161.7 %collective-permute-start.9 = (bf16[256,4096]{1,0:T(8,128)(2,1)}, bf16[256,4096]{1,0:T(8,128)(2,1)}, u32[]{:S(2)}, u32[]{:S(2)}) collective-permute-start(bf16[256,4096]{1,0:T(8,128)(2,1)} %get-tuple-element.127), channel_id=1, source_target_pairs={{0,8},{8,16},{16,24},{24,0},{1,9},{9,17},{17,25},{25,1},{2,10},{10... | collective-permute-start | bytes 6291464 | tf_op jit(solution)/shard_map/ppermute | solution.py:50
  134.7 121.7 %collective-permute-start.10 = (bf16[256,4096]{1,0:T(8,128)(2,1)}, bf16[256,4096]{1,0:T(8,128)(2,1)}, u32[]{:S(2)}, u32[]{:S(2)}) collective-permute-start(bf16[256,4096]{1,0:T(8,128)(2,1)} %get-tuple-element.127), channel_id=1, source_target_pairs={{0,24},{8,0},{16,8},{24,16},{1,25},{9,1},{17,9},{25,17},{2,26},{10... | collective-permute-start | bytes 6291464 | tf_op jit(solution)/shard_map/ppermute | solution.py:50
  137.8 118.6 %collective-permute-start.7 = (bf16[128,4096]{1,0:T(8,128)(2,1)}, bf16[128,4096]{1,0:T(8,128)(2,1)}, u32[]{:S(2)}, u32[]{:S(2)}) collective-permute-start(bf16[128,4096]{1,0:T(8,128)(2,1)} %slice.185), channel_id=1, source_target_pairs={{0,8},{8,16},{16,24},{24,0},{1,9},{9,17},{17,25},{25,1},{2,10},{10... | collective-permute-start | bytes 3145736 | tf_op jit(solution)/shard_map/ppermute | solution.py:66
  157.2 99.2 %collective-permute-start.8 = (bf16[128,4096]{1,0:T(8,128)(2,1)}, bf16[128,4096]{1,0:T(8,128)(2,1)}, u32[]{:S(2)}, u32[]{:S(2)}) collective-permute-start(bf16[128,4096]{1,0:T(8,128)(2,1)} %slice.186), channel_id=1, source_target_pairs={{0,24},{8,0},{16,8},{24,16},{1,25},{9,1},{17,9},{25,17},{2,26},{10... | collective-permute-start | bytes 3145736 | tf_op jit(solution)/shard_map/ppermute | solution.py:67
  279.8 112.6 %reduce-scatter.7.cloned.1.call-start = ((), (), s32[]{:S(2)}) async-start(), calls=%async_computation.6 | async-start | bytes 7077888 | tf_op jit(solution)/shard_map/reduce_scatter | solution.py:106
  280.6 121.6 %all-gather.9.cloned.1.call-start = ((), (), s32[]{:S(2)}) async-start(), calls=%async_computation.13 | async-start | bytes 4718592 | tf_op jit(solution)/shard_map/all_gather | solution.py:54
  281.8 17.2 %collective-permute-start.13 = (bf16[512,512]{1,0:T(8,128)(2,1)S(1)}, bf16[512,512]{1,0:T(8,128)(2,1)S(1)}, u32[]{:S(2)}, u32[]{:S(2)}) collective-permute-start(bf16[512,512]{1,0:T(8,128)(2,1)S(1)} %slice.195), channel_id=1, source_target_pairs={{0,0},{1,11},{2,18},{3,25},{4,4},{5,15},{6,22},{7,29},{8,1},{9,8},... | collective-permute-start | bytes 1572872 | tf_op jit(solution)/shard_map/ppermute | solution.py:53
  299.8 259.9 %reduce-scatter.13.cloned.1.call-start = ((), (), s32[]{:S(2)}) async-start(), calls=%async_computation.9 | async-start | bytes 3538944 | tf_op jit(solution)/shard_map/reduce_scatter | solution.py:106
  299.9 81.0 %collective-permute-start.14 = (bf16[256,4096]{1,0:T(8,128)(2,1)}, bf16[256,4096]{1,0:T(8,128)(2,1)}, u32[]{:S(2)}, u32[]{:S(2)}) collective-permute-start(bf16[256,4096]{1,0:T(8,128)(2,1)} %get-tuple-element.142), channel_id=1, source_target_pairs={{0,8},{8,16},{16,24},{24,0},{1,9},{9,17},{17,25},{25,1},{2,10},{10... | collective-permute-start | bytes 6291464 | tf_op jit(solution)/shard_map/ppermute | solution.py:50
  300.2 83.5 %collective-permute-start.15 = (bf16[256,4096]{1,0:T(8,128)(2,1)}, bf16[256,4096]{1,0:T(8,128)(2,1)}, u32[]{:S(2)}, u32[]{:S(2)}) collective-permute-start(bf16[256,4096]{1,0:T(8,128)(2,1)} %get-tuple-element.142), channel_id=1, source_target_pairs={{0,24},{8,0},{16,8},{24,16},{1,25},{9,1},{17,9},{25,17},{2,26},{10... | collective-permute-start | bytes 6291464 | tf_op jit(solution)/shard_map/ppermute | solution.py:50
  355.5 41.9 %collective-permute-start.11 = (bf16[128,4096]{1,0:T(8,128)(2,1)}, bf16[128,4096]{1,0:T(8,128)(2,1)}, u32[]{:S(2)}, u32[]{:S(2)}) collective-permute-start(bf16[128,4096]{1,0:T(8,128)(2,1)} %slice.193), channel_id=1, source_target_pairs={{0,8},{8,16},{16,24},{24,0},{1,9},{9,17},{17,25},{25,1},{2,10},{10... | collective-permute-start | bytes 3145736 | tf_op jit(solution)/shard_map/ppermute | solution.py:66
  355.5 46.8 %collective-permute-start.12 = (bf16[128,4096]{1,0:T(8,128)(2,1)}, bf16[128,4096]{1,0:T(8,128)(2,1)}, u32[]{:S(2)}, u32[]{:S(2)}) collective-permute-start(bf16[128,4096]{1,0:T(8,128)(2,1)} %slice.194), channel_id=1, source_target_pairs={{0,24},{8,0},{16,8},{24,16},{1,25},{9,1},{17,9},{25,17},{2,26},{10... | collective-permute-start | bytes 3145736 | tf_op jit(solution)/shard_map/ppermute | solution.py:67
  358.2 105.6 %collective-permute-start.18 = (bf16[256,4096]{1,0:T(8,128)(2,1)}, bf16[256,4096]{1,0:T(8,128)(2,1)}, u32[]{:S(2)}, u32[]{:S(2)}) collective-permute-start(bf16[256,4096]{1,0:T(8,128)(2,1)} %get-tuple-element.157), channel_id=1, source_target_pairs={{0,8},{8,16},{16,24},{24,0},{1,9},{9,17},{17,25},{25,1},{2,10},{10... | collective-permute-start | bytes 6291464 | tf_op jit(solution)/shard_map/ppermute | solution.py:50
  380.9 82.9 %collective-permute-start.19 = (bf16[256,4096]{1,0:T(8,128)(2,1)S(1)}, bf16[256,4096]{1,0:T(8,128)(2,1)}, u32[]{:S(2)}, u32[]{:S(2)}) collective-permute-start(bf16[256,4096]{1,0:T(8,128)(2,1)S(1)} %copy-done.5), channel_id=1, source_target_pairs={{0,24},{8,0},{16,8},{24,16},{1,25},{9,1},{17,9},{25,17},{2,26},{10... | collective-permute-start | bytes 6291464 | tf_op jit(solution)/shard_map/ppermute | solution.py:50
  386.1 77.7 %collective-permute-start.16 = (bf16[128,4096]{1,0:T(8,128)(2,1)}, bf16[128,4096]{1,0:T(8,128)(2,1)}, u32[]{:S(2)}, u32[]{:S(2)}) collective-permute-start(bf16[128,4096]{1,0:T(8,128)(2,1)} %slice.203), channel_id=1, source_target_pairs={{0,8},{8,16},{16,24},{24,0},{1,9},{9,17},{17,25},{25,1},{2,10},{10... | collective-permute-start | bytes 3145736 | tf_op jit(solution)/shard_map/ppermute | solution.py:66
  397.4 66.4 %collective-permute-start.17 = (bf16[128,4096]{1,0:T(8,128)(2,1)}, bf16[128,4096]{1,0:T(8,128)(2,1)S(1)}, u32[]{:S(2)}, u32[]{:S(2)}) collective-permute-start(bf16[128,4096]{1,0:T(8,128)(2,1)} %slice.204), channel_id=1, source_target_pairs={{0,24},{8,0},{16,8},{24,16},{1,25},{9,1},{17,9},{25,17},{2,26},{10... | collective-permute-start | bytes 3145736 | tf_op jit(solution)/shard_map/ppermute | solution.py:67
  484.9 77.6 %reduce-scatter.11.cloned.1.call-start = ((), (), s32[]{:S(2)}) async-start(), calls=%async_computation.8 | async-start | bytes 4718592 | tf_op jit(solution)/shard_map/reduce_scatter | solution.py:106
  485.5 95.0 %all-gather.11.cloned.1.call-start = ((), (), s32[]{:S(2)}) async-start(), calls=%async_computation.14 | async-start | bytes 2359296 | tf_op jit(solution)/shard_map/all_gather | solution.py:54
  486.6 8.4 %collective-permute-start.22 = (bf16[512,256]{1,0:T(8,128)(2,1)S(1)}, bf16[512,256]{1,0:T(8,128)(2,1)S(1)}, u32[]{:S(2)}, u32[]{:S(2)}) collective-permute-start(bf16[512,256]{1,0:T(8,128)(2,1)S(1)} %slice.214), channel_id=1, source_target_pairs={{0,0},{1,11},{2,18},{3,25},{4,4},{5,15},{6,22},{7,29},{8,1},{9,8},... | collective-permute-start | bytes 786440 | tf_op jit(solution)/shard_map/ppermute | solution.py:53
  495.7 184.7 %reduce-scatter.15.cloned.1.call-start = ((), (), s32[]{:S(2)}) async-start(), calls=%async_computation.10 | async-start | bytes 1179648 | tf_op jit(solution)/shard_map/reduce_scatter | solution.py:106
  498.4 53.6 %collective-permute-start.23 = (bf16[256,4096]{1,0:T(8,128)(2,1)S(1)}, bf16[256,4096]{1,0:T(8,128)(2,1)}, u32[]{:S(2)}, u32[]{:S(2)}) collective-permute-start(bf16[256,4096]{1,0:T(8,128)(2,1)S(1)} %copy-done.4), channel_id=1, source_target_pairs={{0,8},{8,16},{16,24},{24,0},{1,9},{9,17},{17,25},{25,1},{2,10},{10... | collective-permute-start | bytes 6291464 | tf_op jit(solution)/shard_map/ppermute | solution.py:50
  498.5 53.5 %collective-permute-start.24 = (bf16[256,4096]{1,0:T(8,128)(2,1)S(1)}, bf16[256,4096]{1,0:T(8,128)(2,1)}, u32[]{:S(2)}, u32[]{:S(2)}) collective-permute-start(bf16[256,4096]{1,0:T(8,128)(2,1)S(1)} %copy-done.4), channel_id=1, source_target_pairs={{0,24},{8,0},{16,8},{24,16},{1,25},{9,1},{17,9},{25,17},{2,26},{10... | collective-permute-start | bytes 6291464 | tf_op jit(solution)/shard_map/ppermute | solution.py:50
  535.0 45.5 %collective-permute-start.20 = (bf16[128,4096]{1,0:T(8,128)(2,1)}, bf16[128,4096]{1,0:T(8,128)(2,1)}, u32[]{:S(2)}, u32[]{:S(2)}) collective-permute-start(bf16[128,4096]{1,0:T(8,128)(2,1)} %slice.212), channel_id=1, source_target_pairs={{0,8},{8,16},{16,24},{24,0},{1,9},{9,17},{17,25},{25,1},{2,10},{10... | collective-permute-start | bytes 3145736 | tf_op jit(solution)/shard_map/ppermute | solution.py:66
  535.6 45.0 %collective-permute-start.21 = (bf16[128,4096]{1,0:T(8,128)(2,1)}, bf16[128,4096]{1,0:T(8,128)(2,1)}, u32[]{:S(2)}, u32[]{:S(2)}) collective-permute-start(bf16[128,4096]{1,0:T(8,128)(2,1)} %slice.213), channel_id=1, source_target_pairs={{0,24},{8,0},{16,8},{24,16},{1,25},{9,1},{17,9},{25,17},{2,26},{10... | collective-permute-start | bytes 3145736 | tf_op jit(solution)/shard_map/ppermute | solution.py:67
  554.3 59.6 %collective-permute-start.25 = (bf16[128,4096]{1,0:T(8,128)(2,1)}, bf16[128,4096]{1,0:T(8,128)(2,1)}, u32[]{:S(2)}, u32[]{:S(2)}) collective-permute-start(bf16[128,4096]{1,0:T(8,128)(2,1)} %slice.221), channel_id=1, source_target_pairs={{0,8},{8,16},{16,24},{24,0},{1,9},{9,17},{17,25},{25,1},{2,10},{10... | collective-permute-start | bytes 3145736 | tf_op jit(solution)/shard_map/ppermute | solution.py:66
  557.8 56.2 %collective-permute-start.26 = (bf16[128,4096]{1,0:T(8,128)(2,1)}, bf16[128,4096]{1,0:T(8,128)(2,1)}, u32[]{:S(2)}, u32[]{:S(2)}) collective-permute-start(bf16[128,4096]{1,0:T(8,128)(2,1)} %slice.222), channel_id=1, source_target_pairs={{0,24},{8,0},{16,8},{24,16},{1,25},{9,1},{17,9},{25,17},{2,26},{10... | collective-permute-start | bytes 3145736 | tf_op jit(solution)/shard_map/ppermute | solution.py:67
  628.7 69.2 %reduce-scatter.17.cloned.1.call-start = ((), (), s32[]{:S(2)}) async-start(), calls=%async_computation.11 | async-start | bytes 2359296 | tf_op jit(solution)/shard_map/reduce_scatter | solution.py:106
  632.7 88.0 %collective-permute-start.35 = (bf16[128,768]{0,1:T(8,128)(2,1)S(1)}, bf16[128,768]{0,1:T(8,128)(2,1)S(1)}, u32[]{:S(2)}, u32[]{:S(2)}) collective-permute-start(bf16[128,768]{0,1:T(8,128)(2,1)S(1)} %bitcast.92), channel_id=1, source_target_pairs={{0,4},{1,0},{2,12},{3,8},{4,20},{5,16},{6,28},{7,24},{8,13},{9,9},... | collective-permute-start | bytes 589832 | tf_op jit(solution)/shard_map/ppermute | solution.py:76
  634.9 85.8 %collective-permute-start.36 = (bf16[128,768]{0,1:T(8,128)(2,1)S(1)}, bf16[128,768]{0,1:T(8,128)(2,1)S(1)}, u32[]{:S(2)}, u32[]{:S(2)}) collective-permute-start(bf16[128,768]{0,1:T(8,128)(2,1)S(1)} %bitcast.91), channel_id=1, source_target_pairs={{0,0},{1,4},{2,8},{3,12},{4,16},{5,20},{6,24},{7,28},{8,9},{9,13},... | collective-permute-start | bytes 589832 | tf_op jit(solution)/shard_map/ppermute | solution.py:76
  641.6 80.6 %collective-permute-start.37 = (bf16[128,768]{0,1:T(8,128)(2,1)S(1)}, bf16[128,768]{0,1:T(8,128)(2,1)S(1)}, u32[]{:S(2)}, u32[]{:S(2)}) collective-permute-start(bf16[128,768]{0,1:T(8,128)(2,1)S(1)} %bitcast.90), channel_id=1, source_target_pairs={{0,4},{1,0},{2,12},{3,8},{4,20},{5,16},{6,28},{7,24},{8,13},{9,9},... | collective-permute-start | bytes 589832 | tf_op jit(solution)/shard_map/ppermute | solution.py:76
  652.7 21.8 %collective-permute-start.31 = (bf16[128,512]{0,1:T(8,128)(2,1)S(1)}, bf16[128,512]{0,1:T(8,128)(2,1)S(1)}, u32[]{:S(2)}, u32[]{:S(2)}) collective-permute-start(bf16[128,512]{0,1:T(8,128)(2,1)S(1)} %bitcast.96), channel_id=1, source_target_pairs={{0,4},{1,0},{2,12},{3,8},{4,20},{5,16},{6,28},{7,24},{8,13},{9,9},... | collective-permute-start | bytes 393224 | tf_op jit(solution)/shard_map/ppermute | solution.py:76
  657.5 19.0 %collective-permute-start.32 = (bf16[128,512]{0,1:T(8,128)(2,1)S(1)}, bf16[128,512]{0,1:T(8,128)(2,1)S(1)}, u32[]{:S(2)}, u32[]{:S(2)}) collective-permute-start(bf16[128,512]{0,1:T(8,128)(2,1)S(1)} %bitcast.95), channel_id=1, source_target_pairs={{0,0},{1,4},{2,8},{3,12},{4,16},{5,20},{6,24},{7,28},{8,9},{9,13},... | collective-permute-start | bytes 393224 | tf_op jit(solution)/shard_map/ppermute | solution.py:76
  674.6 8.4 %collective-permute-start.33 = (bf16[128,512]{0,1:T(8,128)(2,1)S(1)}, bf16[128,512]{0,1:T(8,128)(2,1)S(1)}, u32[]{:S(2)}, u32[]{:S(2)}) collective-permute-start(bf16[128,512]{0,1:T(8,128)(2,1)S(1)} %bitcast.94), channel_id=1, source_target_pairs={{0,4},{1,0},{2,12},{3,8},{4,20},{5,16},{6,28},{7,24},{8,13},{9,9},... | collective-permute-start | bytes 393224 | tf_op jit(solution)/shard_map/ppermute | solution.py:76
  676.5 11.2 %collective-permute-start.34 = (bf16[128,512]{0,1:T(8,128)(2,1)S(1)}, bf16[128,512]{0,1:T(8,128)(2,1)S(1)}, u32[]{:S(2)}, u32[]{:S(2)}) collective-permute-start(bf16[128,512]{0,1:T(8,128)(2,1)S(1)} %bitcast.93), channel_id=1, source_target_pairs={{0,0},{1,4},{2,8},{3,12},{4,16},{5,20},{6,24},{7,28},{8,9},{9,13},... | collective-permute-start | bytes 393224 | tf_op jit(solution)/shard_map/ppermute | solution.py:76
  683.0 7.5 %collective-permute-start.27 = (bf16[128,256]{0,1:T(8,128)(2,1)S(1)}, bf16[128,256]{0,1:T(8,128)(2,1)S(1)}, u32[]{:S(2)}, u32[]{:S(2)}) collective-permute-start(bf16[128,256]{0,1:T(8,128)(2,1)S(1)} %get-tuple-element.221), channel_id=1, source_target_pairs={{0,4},{1,0},{2,12},{3,8},{4,20},{5,16},{6,28},{7,24},{8,13},{9,9},... | collective-permute-start | bytes 196616 | tf_op jit(solution)/shard_map/ppermute | solution.py:76
  687.7 9.1 %collective-permute-start.28 = (bf16[128,256]{0,1:T(8,128)(2,1)S(1)}, bf16[128,256]{0,1:T(8,128)(2,1)S(1)}, u32[]{:S(2)}, u32[]{:S(2)}) collective-permute-start(bf16[128,256]{0,1:T(8,128)(2,1)S(1)} %get-tuple-element.220), channel_id=1, source_target_pairs={{0,0},{1,4},{2,8},{3,12},{4,16},{5,20},{6,24},{7,28},{8,9},{9,13},... | collective-permute-start | bytes 196616 | tf_op jit(solution)/shard_map/ppermute | solution.py:76
  699.0 10.5 %collective-permute-start.29 = (bf16[128,256]{0,1:T(8,128)(2,1)S(1)}, bf16[128,256]{0,1:T(8,128)(2,1)S(1)}, u32[]{:S(2)}, u32[]{:S(2)}) collective-permute-start(bf16[128,256]{0,1:T(8,128)(2,1)S(1)} %get-tuple-element.217), channel_id=1, source_target_pairs={{0,4},{1,0},{2,12},{3,8},{4,20},{5,16},{6,28},{7,24},{8,13},{9,9},... | collective-permute-start | bytes 196616 | tf_op jit(solution)/shard_map/ppermute | solution.py:76
  704.0 12.6 %collective-permute-start.30 = (bf16[128,256]{0,1:T(8,128)(2,1)S(1)}, bf16[128,256]{0,1:T(8,128)(2,1)S(1)}, u32[]{:S(2)}, u32[]{:S(2)}) collective-permute-start(bf16[128,256]{0,1:T(8,128)(2,1)S(1)} %get-tuple-element.216), channel_id=1, source_target_pairs={{0,0},{1,4},{2,8},{3,12},{4,16},{5,20},{6,24},{7,28},{8,9},{9,13},... | collective-permute-start | bytes 196616 | tf_op jit(solution)/shard_map/ppermute | solution.py:76
  709.5 12.7 %collective-permute-start.38 = (bf16[128,768]{0,1:T(8,128)(2,1)S(1)}, bf16[128,768]{0,1:T(8,128)(2,1)S(1)}, u32[]{:S(2)}, u32[]{:S(2)}) collective-permute-start(bf16[128,768]{0,1:T(8,128)(2,1)S(1)} %bitcast.89), channel_id=1, source_target_pairs={{0,0},{1,4},{2,8},{3,12},{4,16},{5,20},{6,24},{7,28},{8,9},{9,13},... | collective-permute-start | bytes 589832 | tf_op jit(solution)/shard_map/ppermute | solution.py:76
  (31 other events, 490.9 us)
Sparse Core Ops, SparseCore 0:
  24.3 50.1 all-gather.6
  280.0 42.0 reduce-scatter.8
  324.4 45.4 reduce-scatter.6
  371.4 30.7 all-gather.8
  485.0 32.2 reduce-scatter.12
  519.4 34.3 reduce-scatter.10
  555.5 25.0 all-gather.10
  628.9 32.4 reduce-scatter.14
  663.7 34.1 reduce-scatter.16

commit v2 on v1

v2 whole, which is shorter than its diff:
```python
import functools

import jax
import jax.numpy as jnp
from jax import lax
from jax.experimental import pallas as pl
from jax.experimental.pallas import tpu as pltpu
from jax.sharding import PartitionSpec as P


BLOCK_SIZE = 256
PIECE = 512


def group_kernel(group, halves, has_total, *refs):
    refs = list(refs)
    block_refs = [refs.pop(0) for _ in range(4)]
    panel_ref, side_ref = refs.pop(0), refs.pop(0)
    total_ref = refs.pop(0) if has_total else None
    if has_total:
        refs.pop(0)
    lower_ref, right_ref = refs.pop(0), refs.pop(0)
    next_ref = refs.pop(0) if group else None
    turned, rows = refs
    mesh_rows = len(block_refs)
    size = block_refs[0].shape[0]
    turns = lower_ref.shape[1] // (halves * size)

    def place(idx):
        return slice((idx % halves * turns + idx // halves) * size, (idx % halves * turns + idx // halves + 1) * size)

    @pl.when(pl.program_id(0) == 0)
    def _():
        lower_ref[...] = jnp.zeros_like(lower_ref)
        for idx in range(group + 1):
            for rel in range(mesh_rows):
                tile = panel_ref[idx % halves * mesh_rows + rel, :, idx // halves * size:(idx // halves + 1) * size]
                turned[idx * size:(idx + 1) * size, rel * size:(rel + 1) * size] = tile.T

    for rel in range(mesh_rows):
        rows[rel * size:(rel + 1) * size, :] = block_refs[rel][...]
    for idx in range(group + 1):
        here = slice(idx * size, (idx + 1) * size)
        lower_ref[:, place(idx)] += lax.dot_general(
            rows[...], side_ref[here, :], (((1,), (1,)), ((), ())), preferred_element_type=jnp.float32
        )
        share = jnp.dot(turned[here, :], rows[...], preferred_element_type=jnp.float32)
        if has_total:
            share = total_ref[here, :] + share
        if idx == group:
            right_ref[...] = share.astype(right_ref.dtype)
        else:
            next_ref[here, :] = share


def run_group(group, halves, blocks, panel, side, total, right):
    size = blocks[1].shape[0]
    num_cols = side.shape[1]
    width = (group + 1) * size
    wide = -(-(group + 1) // halves) * halves * size
    depth = panel.shape[1] // halves
    piece = min(PIECE, num_cols)
    has_total = total is not None
    in_specs = [pl.BlockSpec((size, piece), lambda j: (group, j))]
    in_specs += [pl.BlockSpec((size, piece), lambda j: (0, j))] * 3
    in_specs += [
        pl.BlockSpec((panel.shape[0], depth, panel.shape[2]), lambda j: (0, group % halves, 0)),
        pl.BlockSpec((width, piece), lambda j: (0, j)),
    ]
    args = [*blocks, panel, side]
    aliases = {}
    if has_total:
        in_specs += [pl.BlockSpec((width, piece), lambda j: (0, j)), pl.BlockSpec(memory_space=pl.ANY)]
        args += [total, right]
        aliases = {len(args) - 1: 1}
    out_shape = [
        jax.ShapeDtypeStruct((4 * size, wide), jnp.float32),
        jax.ShapeDtypeStruct(side.shape, jnp.bfloat16),
    ]
    out_specs = [
        pl.BlockSpec((4 * size, wide), lambda j: (0, 0)),
        pl.BlockSpec((size, piece), lambda j: (group, j)),
    ]
    if group:
        out_shape.append(jax.ShapeDtypeStruct((group * size, num_cols), jnp.float32))
        out_specs.append(pl.BlockSpec((group * size, piece), lambda j: (0, j)))
    return pl.pallas_call(
        functools.partial(group_kernel, group, halves, has_total),
        grid=(num_cols // piece,),
        in_specs=in_specs,
        out_specs=out_specs,
        out_shape=out_shape,
        scratch_shapes=[pltpu.VMEM((width, 4 * size), jnp.bfloat16), pltpu.VMEM((4 * size, piece), jnp.bfloat16)],
        input_output_aliases=aliases,
        compiler_params=pltpu.CompilerParams(vmem_limit_bytes=56 * 1024 * 1024),
        cost_estimate=pl.CostEstimate(
            flops=4 * 4 * size * width * num_cols, bytes_accessed=num_cols * (12 * size + 10 * width), transcendentals=0
        ),
    )(*args)


def solution(mesh):
    mesh_rows = mesh.shape["row"]
    mesh_cols = mesh.shape["col"]
    halves = mesh_cols // mesh_rows
    block_spec = P(("batch", "row"), "col")
    up = [(row, (row + 1) % mesh_rows) for row in range(mesh_rows)]
    down = [(row, (row - 1) % mesh_rows) for row in range(mesh_rows)]

    spread = []
    collect = [[] for _ in range(halves)]
    for row in range(mesh_rows):
        for col in range(mesh_cols):
            home, half = col % mesh_rows, col // mesh_rows
            spread.append((row * mesh_cols + col, home * mesh_cols + half * mesh_rows + (row - home) % mesh_rows))
            rel, part = col // halves, col % halves
            for turn in range(halves):
                owner = (row + rel) % mesh_rows * mesh_cols + row + mesh_rows * ((part + turn) % halves)
                collect[turn].append((row * mesh_cols + col, owner))

    def shards(lower_tri, right_side, grad_out):
        rows_here, cols_here = lower_tri.shape
        num_groups = rows_here // BLOCK_SIZE
        num_supers = num_groups // halves
        my_col = lax.axis_index("col")
        my_half = my_col // mesh_rows
        my_part = my_col % halves

        own = [grad_out[group * BLOCK_SIZE:(group + 1) * BLOCK_SIZE] for group in range(num_groups)]
        near = {}
        far = {}
        panels = {
            sup: lower_tri[sup * halves * BLOCK_SIZE:(sup + 1) * halves * BLOCK_SIZE, :(sup + 1) * BLOCK_SIZE]
            for sup in range(num_supers)
        }
        totals = {}
        lowers = {}
        sums = {}
        state = {"right": None}

        def send_own(group):
            near[group] = (lax.ppermute(own[group], "row", up), lax.ppermute(own[group], "row", down))

        def spread_panel(sup):
            panel = lax.ppermute(panels[sup], ("row", "col"), spread)
            panels[sup] = lax.all_gather(panel, "col", axis=0)

        def forward(group):
            waits = list(near[group])
            later = group - 2
            if later >= 0:
                waits.append(own[later])
            if group + 2 in totals:
                waits.append(totals[group + 2])
            waits = list(lax.optimization_barrier(tuple(waits)))
            near[group] = (waits.pop(0), waits.pop(0))
            if group % 2:
                far[group] = lax.ppermute(near[group][0], "row", up)
            else:
                far[group] = lax.ppermute(near[group][1], "row", down)
            if later >= 0:
                own[later] = waits.pop(0)
                send_own(later)
            if group + 2 in totals:
                totals[group + 2] = waits.pop(0)

        def choose(values, turn):
            width = values.shape[1] // halves
            chosen = values[:, turn * width:(turn + 1) * width]
            for part in range(1, halves):
                start = (part + turn) % halves * width
                chosen = jnp.where(my_part == part, values[:, start:start + width], chosen)
            return chosen.astype(jnp.bfloat16)

        def collect_lower(sends):
            return [lax.ppermute(send, ("row", "col"), collect[turn]) for turn, send in enumerate(sends)]

        def by_part(turns):
            ordered = []
            for part in range(halves):
                piece = turns[0]
                for turn in range(1, halves):
                    piece = jnp.where((my_half - part) % halves == turn, turns[turn], piece)
                ordered.append(piece)
            return ordered

        def widen(value):
            return jnp.pad(value, ((0, 0), (0, cols_here - value.shape[1])))

        def compute(group):
            sup = group // halves
            waits = [near[group][1], far[group], near[group][0], panels[sup]]
            if group > 0:
                waits += near[group - 1]
            if group + 1 in totals:
                waits.append(totals[group + 1])
            early = range(halves, num_groups)
            if group == 0:
                waits += state["sends"]
            waits = list(lax.optimization_barrier(tuple(waits)))
            blocks, panels[sup] = waits[:3], waits[3]
            waits = waits[4:]
            if group > 0:
                near[group - 1] = (waits.pop(0), waits.pop(0))
            total = waits.pop(0) if group + 1 in totals else None
            if group == 0:
                state["early"] = collect_lower(waits)
            lowers[group], state["right"], *rest = run_group(
                group, halves, [grad_out, *blocks], panels[sup], right_side, total, state["right"]
            )
            if rest:
                totals[group] = rest[0]
            if group in early:
                sums[group] = lax.psum_scatter(lowers[group], "col", scatter_dimension=0, tiled=True)
            if group == halves:
                state["sends"] = [
                    jnp.concatenate([widen(choose(sums[early_group], turn)) for early_group in early], axis=0)
                    for turn in range(halves)
                ]

        for sup in reversed(range(num_supers)):
            spread_panel(sup)
        send_own(num_groups - 1)
        send_own(num_groups - 2)
        forward(num_groups - 1)
        for group in reversed(range(num_groups)):
            if group > 0:
                forward(group - 1)
            compute(group)

        late = jnp.stack([lowers[group].reshape(mesh_rows, BLOCK_SIZE, -1) for group in range(halves)], axis=1)
        late = lax.psum_scatter(late.reshape(rows_here * 2 * mesh_rows // num_groups, -1), "col", scatter_dimension=0, tiled=True)
        late = by_part(collect_lower([choose(late, turn) for turn in range(halves)]))
        half_size = BLOCK_SIZE // halves
        rest = by_part(state["early"])
        lower_rows = [widen(piece) for piece in late]
        for idx in range(num_groups - halves):
            lower_rows += [piece[idx * half_size:(idx + 1) * half_size] for piece in rest]
        grad_lower = jnp.concatenate(lower_rows, axis=0)
        row_pos = jnp.arange(rows_here)[:, None]
        col_pos = jnp.arange(cols_here)[None, :]
        row_global = (row_pos // BLOCK_SIZE * mesh_rows + lax.axis_index("row")) * BLOCK_SIZE + row_pos % BLOCK_SIZE
        col_global = (col_pos // BLOCK_SIZE * mesh_cols + my_col) * BLOCK_SIZE + col_pos % BLOCK_SIZE
        grad_lower = jnp.where(row_global >= col_global, grad_lower, 0.0).astype(jnp.bfloat16)
        return state["right"], grad_lower

    return jax.shard_map(shards, mesh=mesh, in_specs=(block_spec, block_spec, block_spec), out_specs=(block_spec, block_spec), check_vma=False)
```

time: 743 us -> 719 us (0.968)
  waiting for transfers between devices: 158 us -> 455 us
  local copies, waits for them, and re-layouts: 266 us -> 20.8 us
  matrix products: 167 us -> 0 us
  Pallas kernels: 0 us -> 141 us
  starting transfers between devices: 114 us -> 73 us
    dot_general x12 -> x0, matrix products: 167 us -> none  [the longest x6 96.4 us: compute(): lax.dot_general(panel[:, :width], grad_rows, (((0,), (0,)), ((), ())), pr...]
    ppermute x12 -> x6, waiting for transfers between devices: 16.9 us -> 176 us  [the longest x3 127 us: forward(): far[group] = lax.ppermute(near[group][0], 'row', up)]
    pallas_call x0 -> x6, Pallas kernels: none -> 141 us  [run_group(): pl.pallas_call(functools.partial(group_kernel, group, halves, has_total),...]
    reduce_scatter x6 -> x5, waiting for transfers between devices: 0.48 us -> 119 us  [the longest x4 63.6 us: compute(): lax.psum_scatter(lowers[group], 'col', scatter_dimension=0, tiled=True)]
    slice x20 -> x0, local copies, waits for them, and re-layouts: 64.5 us -> none  [the longest x3 39.1 us: compute(): panels[sup]]
    unnamed x106 -> x25, local copies, waits for them, and re-layouts: 64.3 us -> 6.32 us
    reshape x13 -> x0, local copies, waits for them, and re-layouts: 49.4 us -> none  [the longest x4 33.2 us: compute(): panels[sup]]
    ppermute x12 -> x4, starting transfers between devices: 47 us -> 14.5 us  [collect_lower(): lax.ppermute(send, ('row', 'col'), collect[turn])]
  transfers between devices with their start and end apart: 48 -> 33, of which waited for: 16 -> 15; matrix products, arithmetic and copies ran while one was open for 50% -> 3% of each run, Pallas kernels for 0% -> 18%
where the time goes in v2:
time: 719 us; the launch traced here: 717 us
  waiting for transfers between devices  455 us (63%)
  Pallas kernels  141 us (20%)
  starting transfers between devices  73 us (10%)
  local copies, waits for them, and re-layouts  20.8 us (3%)
  between operations  14.5 us (2%)
  other arithmetic  12.7 us (2%)
    pallas_call x6, Pallas kernels, run_group(): pl.pallas_call(functools.partial(group_kernel, group, halves, has_total),...  141 us
    ppermute x3, waiting for transfers between devices, forward(): far[group] = lax.ppermute(near[group][0], 'row', up)  127 us
    ppermute x6, waiting for transfers between devices, send_own(): lax.ppermute(own[group], 'row', up)  98.3 us
    reduce_scatter x4, waiting for transfers between devices, compute(): lax.psum_scatter(lowers[group], 'col', scatter_dimension=0, tiled=True)  63.6 us
    reduce_scatter x1, waiting for transfers between devices, shards(): lax.psum_scatter(late.reshape(rows_here * 2 * mesh_rows // num_groups, -1...  55 us
    ppermute x3, waiting for transfers between devices, spread_panel(): panel = lax.ppermute(panels[sup], ('row', 'col'), spread)  53.7 us
    ppermute x3, waiting for transfers between devices, forward(): far[group] = lax.ppermute(near[group][1], 'row', down)  48.7 us
    ppermute x6, starting transfers between devices, send_own(): lax.ppermute(own[group], 'row', down)  21.5 us
  transfers between devices with their start and end apart: 33, of which 15 were waited for; matrix products, arithmetic and copies ran while one was open for 3% of the time, Pallas kernels for 18%

profile of v2, /device:TPU:97, one launch (start us, length us, event | category | flops | bytes accessed | tf_op | source)
XLA Modules:
  0.0 717.2 jit_solution(12617438540644358761)
XLA Ops:
  7.2 1.2 slice.93
  8.4 5.7 collective-permute-start.3
  14.1 9.1 %collective-permute-done.3 = bf16[512,768]{1,0:T(8,128)(2,1)S(1)} collective-permute-done((bf16[512,768]{1,0:T(8,128)(2,1)S(1)}, bf16[512,768]{1,0:T(8,128)(2,1)S(1)}, u32[]{:S(2)}, u32[]{:S(2)}) %collective-permute-start.3) | collective-permute-done | bytes 786464 | tf_op jit(solution)/shard_map/ppermute | solution.py:145
  25.3 5.4 collective-permute-start.10
  30.7 6.2 collective-permute-done.10
  37.8 8.4 %fusion.33 = (bf16[256,4096]{1,0:T(8,128)(2,1)S(1)}, bf16[256,4096]{1,0:T(8,128)(2,1)}, bf16[256,4096]{1,0:T(8,128)(2,1)}, bf16[256,4096]{1,0:T(8,128)(2,1)}, bf...) fusion(bf16[1536,4096]{1,0:T(8,128)(2,1)} %refs_0_.11), kind=kLoop, calls=%fused_computation.70 | loop fusion | bytes 25165824 | tf_op jit(solution)/shard_map/slice | solution.py:129
  46.2 10.6 %collective-permute-start = (bf16[256,4096]{1,0:T(8,128)(2,1)S(1)}, bf16[256,4096]{1,0:T(8,128)(2,1)}, u32[]{:S(2)}, u32[]{:S(2)}) collective-permute-start(bf16[256,4096]{1,0:T(8,128)(2,1)S(1)} %get-tuple-element.163), channel_id=1, source_target_pairs={{0,8},{8,16},{16,24},{24,0},{1,9},{9,17},{17,25},{25,1},{2,10},{10... | collective-permute-start | bytes 6291464 | tf_op jit(solution)/shard_map/ppermute | solution.py:142
  56.8 12.2 %collective-permute-start.1 = (bf16[256,4096]{1,0:T(8,128)(2,1)S(1)}, bf16[256,4096]{1,0:T(8,128)(2,1)S(1)}, u32[]{:S(2)}, u32[]{:S(2)}) collective-permute-start(bf16[256,4096]{1,0:T(8,128)(2,1)S(1)} %get-tuple-element.163), channel_id=1, source_target_pairs={{0,24},{8,0},{16,8},{24,16},{1,25},{9,1},{17,9},{25,17},{2,26},{10... | collective-permute-start | bytes 6291464 | tf_op jit(solution)/shard_map/ppermute | solution.py:142
  69.0 2.7 collective-permute-start.5
  71.7 43.5 %collective-permute-done.refs_3_ = bf16[256,4096]{1,0:T(8,128)(2,1)} collective-permute-done((bf16[256,4096]{1,0:T(8,128)(2,1)S(1)}, bf16[256,4096]{1,0:T(8,128)(2,1)}, u32[]{:S(2)}, u32[]{:S(2)}) %collective-permute-start) | collective-permute-done | bytes 2097184 | tf_op jit(solution)/shard_map/ppermute | solution.py:142
  117.0 2.3 collective-permute-start.17
  119.3 38.5 %collective-permute-done.17 = bf16[512,256]{1,0:T(8,128)(2,1)S(1)} collective-permute-done((bf16[512,256]{1,0:T(8,128)(2,1)S(1)}, bf16[512,256]{1,0:T(8,128)(2,1)S(1)}, u32[]{:S(2)}, u32[]{:S(2)}) %collective-permute-start.17) | collective-permute-done | bytes 262176 | tf_op jit(solution)/shard_map/ppermute | solution.py:145
  158.6 4.9 collective-permute-start.7
  163.6 1.5 collective-permute-start.11
  165.0 1.3 collective-permute-start.12
  166.3 38.7 %collective-permute-done.2.refs_2_ = bf16[256,4096]{1,0:T(8,128)(2,1)} collective-permute-done((bf16[256,4096]{1,0:T(8,128)(2,1)}, bf16[256,4096]{1,0:T(8,128)(2,1)}, u32[]{:S(2)}, u32[]{:S(2)}) %collective-permute-start.2) | collective-permute-done | bytes 2097184 | tf_op jit(solution)/shard_map/ppermute | solution.py:158
  205.1 1.5 collective-permute-start.6
  206.5 35.0 %shard_map.50 = (f32[1024,1536]{1,0:T(8,128)}, bf16[1536,4096]{1,0:T(8,128)(2,1)}, f32[1280,4096]{1,0:T(8,128)}) custom-call(bf16[1536,4096]{1,0:T(8,128)(2,1)} %refs_0_.11, bf16[256,4096]{1,0:T(8,128)(2,1)} %copy-done.7, bf16[256,4096]{1,0:T(8,128)(2,1)} %collective-permute-done.2.refs_2_, bf16[256,4096]{1,0:T(8,128)(2,1)} %collective-permute-done.refs_3_, ...), custom_call_target="tpu_custom_call" | custom-call | flops 25769803776 | bytes 75497472 | tf_op jit(solution)/shard_map/pallas_call | solution.py:87
  241.5 8.5 %collective-permute-done.7.refs_3_ = bf16[256,4096]{1,0:T(8,128)(2,1)} collective-permute-done((bf16[256,4096]{1,0:T(8,128)(2,1)}, bf16[256,4096]{1,0:T(8,128)(2,1)}, u32[]{:S(2)}, u32[]{:S(2)}) %collective-permute-start.7) | collective-permute-done | bytes 2097184 | tf_op jit(solution)/shard_map/ppermute | solution.py:142
  250.0 2.7 collective-permute-start.15
  252.7 48.7 %collective-permute-done.6.refs_2_ = bf16[256,4096]{1,0:T(8,128)(2,1)} collective-permute-done((bf16[256,4096]{1,0:T(8,128)(2,1)}, bf16[256,4096]{1,0:T(8,128)(2,1)}, u32[]{:S(2)}, u32[]{:S(2)}) %collective-permute-start.6) | collective-permute-done | bytes 2097184 | tf_op jit(solution)/shard_map/ppermute | solution.py:160
  301.5 31.3 %shard_map.51 = (f32[1024,1536]{1,0:T(8,128)}, bf16[1536,4096]{1,0:T(8,128)(2,1)}, f32[1024,4096]{1,0:T(8,128)}) custom-call(bf16[1536,4096]{1,0:T(8,128)(2,1)} %refs_0_.11, bf16[256,4096]{1,0:T(8,128)(2,1)} %collective-permute-done.5.refs_1_, bf16[256,4096]{1,0:T(8,128)(2,1)} %collective-permute-done.6.refs_2_, ...), custom_call_target="tpu_custom_call", output_to_operand_aliasing={{1}: (7, {})} | custom-call | flops 21474836480 | bytes 65011712 | tf_op jit(solution)/shard_map/pallas_call | solution.py:87
  332.8 2.9 collective-permute-start.13
  335.7 46.6 %collective-permute-done.9.refs_2_ = bf16[256,4096]{1,0:T(8,128)(2,1)} collective-permute-done((bf16[256,4096]{1,0:T(8,128)(2,1)}, bf16[256,4096]{1,0:T(8,128)(2,1)}, u32[]{:S(2)}, u32[]{:S(2)}) %collective-permute-start.9) | collective-permute-done | bytes 2097184 | tf_op jit(solution)/shard_map/ppermute | solution.py:158
  382.3 25.4 %shard_map.52 = (f32[1024,1024]{1,0:T(8,128)}, bf16[1536,4096]{1,0:T(8,128)(2,1)}, f32[768,4096]{1,0:T(8,128)}) custom-call(bf16[1536,4096]{1,0:T(8,128)(2,1)} %refs_0_.11, bf16[256,4096]{1,0:T(8,128)(2,1)} %collective-permute-done.8.refs_1_, bf16[256,4096]{1,0:T(8,128)(2,1)} %collective-permute-done.9.refs_2_, ...), custom_call_target="tpu_custom_call", output_to_operand_aliasing={{1}: (7, {})} | custom-call | flops 17179869184 | bytes 54525952 | tf_op jit(solution)/shard_map/pallas_call | solution.py:87
  407.7 21.0 %shard_map.53 = (f32[1024,1024]{1,0:T(8,128)}, bf16[1536,4096]{1,0:T(8,128)(2,1)}, f32[512,4096]{1,0:T(8,128)}) custom-call(bf16[1536,4096]{1,0:T(8,128)(2,1)} %refs_0_.11, bf16[256,4096]{1,0:T(8,128)(2,1)} %collective-permute-done.12.refs_1_, bf16[256,4096]{1,0:T(8,128)(2,1)} %collective-permute-done.13.refs_2_, ...), custom_call_target="tpu_custom_call", output_to_operand_aliasing={{1}: (7, {})} | custom-call | flops 12884901888 | bytes 44040192 | tf_op jit(solution)/shard_map/pallas_call | solution.py:87
  431.1 2.6 collective-permute-start.19
  433.7 46.3 %collective-permute-done.18.refs_3_ = bf16[256,4096]{1,0:T(8,128)(2,1)S(1)} collective-permute-done((bf16[256,4096]{1,0:T(8,128)(2,1)S(1)}, bf16[256,4096]{1,0:T(8,128)(2,1)S(1)}, u32[]{:S(2)}, u32[]{:S(2)}) %collective-permute-start.18) | collective-permute-done | bytes 2097184 | tf_op jit(solution)/shard_map/ppermute | solution.py:142
  480.0 1.4 copy-done
  482.2 41.6 %collective-permute-done.16.refs_2_ = bf16[256,4096]{1,0:T(8,128)(2,1)} collective-permute-done((bf16[256,4096]{1,0:T(8,128)(2,1)}, bf16[256,4096]{1,0:T(8,128)(2,1)}, u32[]{:S(2)}, u32[]{:S(2)}) %collective-permute-start.16) | collective-permute-done | bytes 2097184 | tf_op jit(solution)/shard_map/ppermute | solution.py:158
  523.8 16.3 %shard_map.54 = (f32[1024,512]{1,0:T(8,128)}, bf16[1536,4096]{1,0:T(8,128)(2,1)}, f32[256,4096]{1,0:T(8,128)}) custom-call(bf16[1536,4096]{1,0:T(8,128)(2,1)} %refs_0_.11, bf16[256,4096]{1,0:T(8,128)(2,1)} %collective-permute-done.15.refs_1_, bf16[256,4096]{1,0:T(8,128)(2,1)} %collective-permute-done.16.refs_2_, ...), custom_call_target="tpu_custom_call", output_to_operand_aliasing={{1}: (7, {})} | custom-call | flops 8589934592 | bytes 33554432 | tf_op jit(solution)/shard_map/pallas_call | solution.py:87
  541.2 1.8 select_convert_fusion.6
  543.0 22.7 %reduce-scatter.10.cloned.1.call-done = f32[128,1536]{1,0:T(8,128)} async-done(((f32[1024,1536]{1,0:T(8,128)}), f32[128,1536]{1,0:T(8,128)}) %reduce-scatter.10.cloned.1.call-update) | async-done | bytes 786448 | tf_op jit(solution)/shard_map/reduce_scatter | solution.py:214
  565.7 1.2 select_convert_fusion.1
  566.9 40.8 %reduce-scatter.12.cloned.1.call-done = f32[128,1536]{1,0:T(8,128)} async-done(((f32[1024,1536]{1,0:T(8,128)}), f32[128,1536]{1,0:T(8,128)}) %reduce-scatter.12.cloned.1.call-update) | async-done | bytes 786448 | tf_op jit(solution)/shard_map/reduce_scatter | solution.py:214
  608.9 2.0 fusion.7
  610.8 1.3 copy-done.1
  612.1 12.4 %shard_map.55 = (f32[1024,512]{1,0:T(8,128)}, bf16[1536,4096]{1,0:T(8,128)(2,1)}) custom-call(bf16[1536,4096]{1,0:T(8,128)(2,1)} %refs_0_.11, bf16[256,4096]{1,0:T(8,128)(2,1)} %collective-permute-done.19.refs_1_, bf16[256,4096]{1,0:T(8,128)(2,1)} %copy-done.1, bf16[256,4096]{1,0:T(8,128)(2,1)} %copy-done, ...), custom_call_target="tpu_custom_call", output_to_operand_aliasing={{1}: (7, {})} | custom-call | flops 4294967296 | bytes 23068672 | tf_op jit(solution)/shard_map/pallas_call | solution.py:87
  624.5 2.3 pad_maximum_fusion
  626.9 2.8 copy.10
  630.8 3.1 collective-permute-start.23
  633.9 5.5 collective-permute-start.24
  639.5 55.0 %reduce-scatter.14.cloned.1.call-done = f32[256,512]{1,0:T(8,128)} async-done(((f32[2048,512]{1,0:T(8,128)}), f32[256,512]{1,0:T(8,128)}) %reduce-scatter.14.cloned.1.call-update) | async-done | bytes 524304 | tf_op jit(solution)/shard_map/reduce_scatter | solution.py:232
  695.5 3.9 collective-permute-start.21
  699.4 2.0 collective-permute-start.22
  701.5 3.3 collective-permute-done.21
  704.8 3.2 collective-permute-done.22
  708.3 2.0 compare_select_fusion
  (75 shorter events, 13.8 us)
Async XLA Ops:
  7.2 199.4 %all-gather.7.cloned.1.call-start = ((), (), s32[]{:S(2)}) async-start(), calls=%async_computation.10 | async-start | bytes 7077888 | tf_op jit(solution)/shard_map/all_gather | solution.py:146
  8.4 14.8 %collective-permute-start.3 = (bf16[512,768]{1,0:T(8,128)(2,1)S(1)}, bf16[512,768]{1,0:T(8,128)(2,1)S(1)}, u32[]{:S(2)}, u32[]{:S(2)}) collective-permute-start(bf16[512,768]{1,0:T(8,128)(2,1)S(1)} %slice.93), channel_id=1, source_target_pairs={{0,0},{1,11},{2,18},{3,25},{4,4},{5,15},{6,22},{7,29},{8,1},{9,8},... | collective-permute-start | bytes 2359304 | tf_op jit(solution)/shard_map/ppermute | solution.py:145
  23.2 0.9 copy-start.3
  24.2 311.5 %all-gather.9.cloned.1.call-start = ((), (), s32[]{:S(2)}) async-start(), calls=%async_computation.11 | async-start | bytes 4718592 | tf_op jit(solution)/shard_map/all_gather | solution.py:146
  25.3 11.5 %collective-permute-start.10 = (bf16[512,512]{1,0:T(8,128)(2,1)S(1)}, bf16[512,512]{1,0:T(8,128)(2,1)S(1)}, u32[]{:S(2)}, u32[]{:S(2)}) collective-permute-start(bf16[512,512]{1,0:T(8,128)(2,1)S(1)} %slice.97), channel_id=1, source_target_pairs={{0,0},{1,11},{2,18},{3,25},{4,4},{5,15},{6,22},{7,29},{8,1},{9,8},... | collective-permute-start | bytes 1572872 | tf_op jit(solution)/shard_map/ppermute | solution.py:145
  36.8 0.8 copy-start.5
  37.7 444.5 %all-gather.11.cloned.1.call-start = ((), (), s32[]{:S(2)}) async-start(), calls=%async_computation.12 | async-start | bytes 2359296 | tf_op jit(solution)/shard_map/all_gather | solution.py:146
  46.2 69.0 %collective-permute-start = (bf16[256,4096]{1,0:T(8,128)(2,1)S(1)}, bf16[256,4096]{1,0:T(8,128)(2,1)}, u32[]{:S(2)}, u32[]{:S(2)}) collective-permute-start(bf16[256,4096]{1,0:T(8,128)(2,1)S(1)} %get-tuple-element.163), channel_id=1, source_target_pairs={{0,8},{8,16},{16,24},{24,0},{1,9},{9,17},{17,25},{25,1},{2,10},{10... | collective-permute-start | bytes 6291464 | tf_op jit(solution)/shard_map/ppermute | solution.py:142
  56.8 58.4 %collective-permute-start.1 = (bf16[256,4096]{1,0:T(8,128)(2,1)S(1)}, bf16[256,4096]{1,0:T(8,128)(2,1)S(1)}, u32[]{:S(2)}, u32[]{:S(2)}) collective-permute-start(bf16[256,4096]{1,0:T(8,128)(2,1)S(1)} %get-tuple-element.163), channel_id=1, source_target_pairs={{0,24},{8,0},{16,8},{24,16},{1,25},{9,1},{17,9},{25,17},{2,26},{10... | collective-permute-start | bytes 6291464 | tf_op jit(solution)/shard_map/ppermute | solution.py:142
  69.0 94.6 %collective-permute-start.4 = (bf16[256,4096]{1,0:T(8,128)(2,1)}, bf16[256,4096]{1,0:T(8,128)(2,1)}, u32[]{:S(2)}, u32[]{:S(2)}) collective-permute-start(bf16[256,4096]{1,0:T(8,128)(2,1)} %get-tuple-element.161), channel_id=1, source_target_pairs={{0,8},{8,16},{16,24},{24,0},{1,9},{9,17},{17,25},{25,1},{2,10},{10... | collective-permute-start | bytes 6291464 | tf_op jit(solution)/shard_map/ppermute | solution.py:142
  69.0 94.6 %collective-permute-start.5 = (bf16[256,4096]{1,0:T(8,128)(2,1)}, bf16[256,4096]{1,0:T(8,128)(2,1)}, u32[]{:S(2)}, u32[]{:S(2)}) collective-permute-start(bf16[256,4096]{1,0:T(8,128)(2,1)} %get-tuple-element.161), channel_id=1, source_target_pairs={{0,24},{8,0},{16,8},{24,16},{1,25},{9,1},{17,9},{25,17},{2,26},{10... | collective-permute-start | bytes 6291464 | tf_op jit(solution)/shard_map/ppermute | solution.py:142
  115.2 4.1 copy-start.7
  115.2 89.9 %collective-permute-start.2 = (bf16[256,4096]{1,0:T(8,128)(2,1)}, bf16[256,4096]{1,0:T(8,128)(2,1)}, u32[]{:S(2)}, u32[]{:S(2)}) collective-permute-start(bf16[256,4096]{1,0:T(8,128)(2,1)} %collective-permute-done.refs_3_), channel_id=1, source_target_pairs={{0,8},{8,16},{16,24},{24,0},{1,9},{9,17},{17,25},{25,1},{2,10},{10... | collective-permute-start | bytes 6291464 | tf_op jit(solution)/shard_map/ppermute | solution.py:158
  117.0 40.8 %collective-permute-start.17 = (bf16[512,256]{1,0:T(8,128)(2,1)S(1)}, bf16[512,256]{1,0:T(8,128)(2,1)S(1)}, u32[]{:S(2)}, u32[]{:S(2)}) collective-permute-start(bf16[512,256]{1,0:T(8,128)(2,1)S(1)} %slice.99), channel_id=1, source_target_pairs={{0,0},{1,11},{2,18},{3,25},{4,4},{5,15},{6,22},{7,29},{8,1},{9,8},... | collective-permute-start | bytes 786440 | tf_op jit(solution)/shard_map/ppermute | solution.py:145
  157.8 0.7 copy-start.6
  158.6 381.5 %reduce-scatter.6.cloned.1.call-start = ((), (), s32[]{:S(2)}) async-start(), calls=%async_computation.5 | async-start | bytes 4718592 | tf_op jit(solution)/shard_map/reduce_scatter | solution.py:214
  158.6 91.4 %collective-permute-start.7 = (bf16[256,4096]{1,0:T(8,128)(2,1)}, bf16[256,4096]{1,0:T(8,128)(2,1)}, u32[]{:S(2)}, u32[]{:S(2)}) collective-permute-start(bf16[256,4096]{1,0:T(8,128)(2,1)} %get-tuple-element.87), channel_id=1, source_target_pairs={{0,8},{8,16},{16,24},{24,0},{1,9},{9,17},{17,25},{25,1},{2,10},{10... | collective-permute-start | bytes 6291464 | tf_op jit(solution)/shard_map/ppermute | solution.py:142
  163.6 86.5 %collective-permute-start.8 = (bf16[256,4096]{1,0:T(8,128)(2,1)}, bf16[256,4096]{1,0:T(8,128)(2,1)}, u32[]{:S(2)}, u32[]{:S(2)}) collective-permute-start(bf16[256,4096]{1,0:T(8,128)(2,1)} %get-tuple-element.87), channel_id=1, source_target_pairs={{0,24},{8,0},{16,8},{24,16},{1,25},{9,1},{17,9},{25,17},{2,26},{10... | collective-permute-start | bytes 6291464 | tf_op jit(solution)/shard_map/ppermute | solution.py:142
  163.6 169.2 %collective-permute-start.11 = (bf16[256,4096]{1,0:T(8,128)(2,1)}, bf16[256,4096]{1,0:T(8,128)(2,1)}, u32[]{:S(2)}, u32[]{:S(2)}) collective-permute-start(bf16[256,4096]{1,0:T(8,128)(2,1)} %get-tuple-element.97), channel_id=1, source_target_pairs={{0,8},{8,16},{16,24},{24,0},{1,9},{9,17},{17,25},{25,1},{2,10},{10... | collective-permute-start | bytes 6291464 | tf_op jit(solution)/shard_map/ppermute | solution.py:142
  165.0 167.7 %collective-permute-start.12 = (bf16[256,4096]{1,0:T(8,128)(2,1)}, bf16[256,4096]{1,0:T(8,128)(2,1)}, u32[]{:S(2)}, u32[]{:S(2)}) collective-permute-start(bf16[256,4096]{1,0:T(8,128)(2,1)} %get-tuple-element.97), channel_id=1, source_target_pairs={{0,24},{8,0},{16,8},{24,16},{1,25},{9,1},{17,9},{25,17},{2,26},{10... | collective-permute-start | bytes 6291464 | tf_op jit(solution)/shard_map/ppermute | solution.py:142
  205.1 96.3 %collective-permute-start.6 = (bf16[256,4096]{1,0:T(8,128)(2,1)}, bf16[256,4096]{1,0:T(8,128)(2,1)}, u32[]{:S(2)}, u32[]{:S(2)}) collective-permute-start(bf16[256,4096]{1,0:T(8,128)(2,1)} %collective-permute-done.5.refs_1_), channel_id=1, source_target_pairs={{0,24},{8,0},{16,8},{24,16},{1,25},{9,1},{17,9},{25,17},{2,26},{10... | collective-permute-start | bytes 6291464 | tf_op jit(solution)/shard_map/ppermute | solution.py:160
  250.0 157.7 %collective-permute-start.14 = (bf16[256,4096]{1,0:T(8,128)(2,1)}, bf16[256,4096]{1,0:T(8,128)(2,1)}, u32[]{:S(2)}, u32[]{:S(2)}) collective-permute-start(bf16[256,4096]{1,0:T(8,128)(2,1)} %get-tuple-element.111), channel_id=1, source_target_pairs={{0,8},{8,16},{16,24},{24,0},{1,9},{9,17},{17,25},{25,1},{2,10},{10... | collective-permute-start | bytes 6291464 | tf_op jit(solution)/shard_map/ppermute | solution.py:142
  250.0 157.7 %collective-permute-start.15 = (bf16[256,4096]{1,0:T(8,128)(2,1)}, bf16[256,4096]{1,0:T(8,128)(2,1)}, u32[]{:S(2)}, u32[]{:S(2)}) collective-permute-start(bf16[256,4096]{1,0:T(8,128)(2,1)} %get-tuple-element.111), channel_id=1, source_target_pairs={{0,24},{8,0},{16,8},{24,16},{1,25},{9,1},{17,9},{25,17},{2,26},{10... | collective-permute-start | bytes 6291464 | tf_op jit(solution)/shard_map/ppermute | solution.py:142
  301.4 80.9 %collective-permute-start.9 = (bf16[256,4096]{1,0:T(8,128)(2,1)}, bf16[256,4096]{1,0:T(8,128)(2,1)}, u32[]{:S(2)}, u32[]{:S(2)}) collective-permute-start(bf16[256,4096]{1,0:T(8,128)(2,1)} %collective-permute-done.7.refs_3_), channel_id=1, source_target_pairs={{0,8},{8,16},{16,24},{24,0},{1,9},{9,17},{17,25},{25,1},{2,10},{10... | collective-permute-start | bytes 6291464 | tf_op jit(solution)/shard_map/ppermute | solution.py:158
  332.8 74.9 %collective-permute-start.13 = (bf16[256,4096]{1,0:T(8,128)(2,1)}, bf16[256,4096]{1,0:T(8,128)(2,1)}, u32[]{:S(2)}, u32[]{:S(2)}) collective-permute-start(bf16[256,4096]{1,0:T(8,128)(2,1)} %collective-permute-done.12.refs_1_), channel_id=1, source_target_pairs={{0,24},{8,0},{16,8},{24,16},{1,25},{9,1},{17,9},{25,17},{2,26},{10... | collective-permute-start | bytes 6291464 | tf_op jit(solution)/shard_map/ppermute | solution.py:160
  428.8 112.4 %reduce-scatter.8.cloned.1.call-start = ((), (), s32[]{:S(2)}) async-start(), calls=%async_computation.6 | async-start | bytes 4718592 | tf_op jit(solution)/shard_map/reduce_scatter | solution.py:214
  429.4 136.3 %reduce-scatter.10.cloned.1.call-start = ((), (), s32[]{:S(2)}) async-start(), calls=%async_computation.7 | async-start | bytes 7077888 | tf_op jit(solution)/shard_map/reduce_scatter | solution.py:214
  430.1 177.6 %reduce-scatter.12.cloned.1.call-start = ((), (), s32[]{:S(2)}) async-start(), calls=%async_computation.8 | async-start | bytes 7077888 | tf_op jit(solution)/shard_map/reduce_scatter | solution.py:214
  430.9 263.6 %reduce-scatter.14.cloned.1.call-start = ((), (), s32[]{:S(2)}) async-start(), calls=%async_computation.9 | async-start | bytes 4718592 | tf_op jit(solution)/shard_map/reduce_scatter | solution.py:232
  431.0 49.0 %collective-permute-start.18 = (bf16[256,4096]{1,0:T(8,128)(2,1)S(1)}, bf16[256,4096]{1,0:T(8,128)(2,1)S(1)}, u32[]{:S(2)}, u32[]{:S(2)}) collective-permute-start(bf16[256,4096]{1,0:T(8,128)(2,1)S(1)} %get-tuple-element.123), channel_id=1, source_target_pairs={{0,8},{8,16},{16,24},{24,0},{1,9},{9,17},{17,25},{25,1},{2,10},{10... | collective-permute-start | bytes 6291464 | tf_op jit(solution)/shard_map/ppermute | solution.py:142
  431.1 48.9 %collective-permute-start.19 = (bf16[256,4096]{1,0:T(8,128)(2,1)S(1)}, bf16[256,4096]{1,0:T(8,128)(2,1)}, u32[]{:S(2)}, u32[]{:S(2)}) collective-permute-start(bf16[256,4096]{1,0:T(8,128)(2,1)S(1)} %get-tuple-element.123), channel_id=1, source_target_pairs={{0,24},{8,0},{16,8},{24,16},{1,25},{9,1},{17,9},{25,17},{2,26},{10... | collective-permute-start | bytes 6291464 | tf_op jit(solution)/shard_map/ppermute | solution.py:142
  433.7 90.1 %collective-permute-start.16 = (bf16[256,4096]{1,0:T(8,128)(2,1)}, bf16[256,4096]{1,0:T(8,128)(2,1)}, u32[]{:S(2)}, u32[]{:S(2)}) collective-permute-start(bf16[256,4096]{1,0:T(8,128)(2,1)} %collective-permute-done.14.refs_3_), channel_id=1, source_target_pairs={{0,8},{8,16},{16,24},{24,0},{1,9},{9,17},{17,25},{25,1},{2,10},{10... | collective-permute-start | bytes 6291464 | tf_op jit(solution)/shard_map/ppermute | solution.py:158
  480.0 1.4 copy-start
  481.4 129.4 %collective-permute-start.20 = (bf16[256,4096]{1,0:T(8,128)(2,1)}, bf16[256,4096]{1,0:T(8,128)(2,1)S(1)}, u32[]{:S(2)}, u32[]{:S(2)}) collective-permute-start(bf16[256,4096]{1,0:T(8,128)(2,1)} %collective-permute-done.19.refs_1_), channel_id=1, source_target_pairs={{0,24},{8,0},{16,8},{24,16},{1,25},{9,1},{17,9},{25,17},{2,26},{10... | collective-permute-start | bytes 6291464 | tf_op jit(solution)/shard_map/ppermute | solution.py:160
  610.8 1.3 copy-start.1
  612.1 12.4 %copy-start.2 = (f32[1024,512]{1,0:T(8,128)S(1)}, f32[1024,512]{1,0:T(8,128)}, u32[]{:S(2)}) copy-start(f32[1024,512]{1,0:T(8,128)} %get-tuple-element.155) | copy-start | bytes 6291460
  629.6 1.1 copy-start.4
  630.8 70.6 %collective-permute-start.23 = (bf16[512,768]{1,0:T(8,128)(2,1)S(1)}, bf16[512,768]{1,0:T(8,128)(2,1)S(1)}, u32[]{:S(2)}, u32[]{:S(2)}) collective-permute-start(bf16[512,768]{1,0:T(8,128)(2,1)S(1)} %copy-done.4), channel_id=1, source_target_pairs={{0,4},{1,0},{2,12},{3,8},{4,20},{5,16},{6,28},{7,24},{8,13},{9,9},... | collective-permute-start | bytes 2359304 | tf_op jit(solution)/shard_map/ppermute | solution.py:176
  633.9 67.5 %collective-permute-start.24 = (bf16[512,768]{1,0:T(8,128)(2,1)S(1)}, bf16[512,768]{1,0:T(8,128)(2,1)S(1)}, u32[]{:S(2)}, u32[]{:S(2)}) collective-permute-start(bf16[512,768]{1,0:T(8,128)(2,1)S(1)} %get-tuple-element.157), channel_id=1, source_target_pairs={{0,0},{1,4},{2,8},{3,12},{4,16},{5,20},{6,24},{7,28},{8,9},{9,13},... | collective-permute-start | bytes 2359304 | tf_op jit(solution)/shard_map/ppermute | solution.py:176
  695.5 9.3 %collective-permute-start.21 = (bf16[256,256]{1,0:T(8,128)(2,1)S(1)}, bf16[256,256]{1,0:T(8,128)(2,1)S(1)}, u32[]{:S(2)}, u32[]{:S(2)}) collective-permute-start(bf16[256,256]{1,0:T(8,128)(2,1)S(1)} %get-tuple-element.171), channel_id=1, source_target_pairs={{0,4},{1,0},{2,12},{3,8},{4,20},{5,16},{6,28},{7,24},{8,13},{9,9},... | collective-permute-start | bytes 393224 | tf_op jit(solution)/shard_map/ppermute | solution.py:176
  699.4 8.6 %collective-permute-start.22 = (bf16[256,256]{1,0:T(8,128)(2,1)S(1)}, bf16[256,256]{1,0:T(8,128)(2,1)S(1)}, u32[]{:S(2)}, u32[]{:S(2)}) collective-permute-start(bf16[256,256]{1,0:T(8,128)(2,1)S(1)} %get-tuple-element.170), channel_id=1, source_target_pairs={{0,0},{1,4},{2,8},{3,12},{4,16},{5,20},{6,24},{7,28},{8,9},{9,13},... | collective-permute-start | bytes 393224 | tf_op jit(solution)/shard_map/ppermute | solution.py:176
Sparse Core Ops, SparseCore 0:
  24.3 54.5 all-gather.6
  80.5 32.4 all-gather.8
  158.7 82.6 all-gather.10
  428.9 56.3 reduce-scatter.5
  487.4 35.1 reduce-scatter.7
  524.9 40.7 reduce-scatter.9
  568.0 39.6 reduce-scatter.11
  629.8 64.6 reduce-scatter.13

commit v3 on v2

--- a/solution.py
+++ b/solution.py
@@ -10,6 +10,11 @@
 
 BLOCK_SIZE = 256
 PIECE = 512
+LATE_PIECE = 1024
+
+
+def seat(rel, mesh_rows):
+    return rel % 2 * (mesh_rows // 2) + rel // 2
 
 
 def group_kernel(group, halves, has_total, *refs):
@@ -34,7 +39,7 @@
         lower_ref[...] = jnp.zeros_like(lower_ref)
         for idx in range(group + 1):
             for rel in range(mesh_rows):
-                tile = panel_ref[idx % halves * mesh_rows + rel, :, idx // halves * size:(idx // halves + 1) * size]
+                tile = panel_ref[idx % halves * mesh_rows + seat(rel, mesh_rows), :, idx // halves * size:(idx // halves + 1) * size]
                 turned[idx * size:(idx + 1) * size, rel * size:(rel + 1) * size] = tile.T
 
     for rel in range(mesh_rows):
@@ -99,6 +104,112 @@
     )(*args)
 
 
+def turn_panel(panel_ref, turned, rels, halves, mesh_rows):
+    depth, size = panel_ref.shape[1], panel_ref.shape[2]
+    for idx in range(halves):
+        for turn, rel in enumerate(rels):
+            for part in range(depth // size):
+                tile = panel_ref[idx * mesh_rows + seat(rel, mesh_rows), part * size:(part + 1) * size, :]
+                start = turn * depth + part * size
+                turned[idx * size:(idx + 1) * size, start:start + size] = tile.T
+
+
+def late_near_kernel(halves, own_ref, next_refs, prev_refs, panel_ref, side_ref, total_ref, lower_ref, sum_ref, turned, rows):
+    mesh_rows = panel_ref.shape[0] // halves
+    depth, size = panel_ref.shape[1], panel_ref.shape[2]
+    last = mesh_rows - 1
+
+    @pl.when(pl.program_id(0) == 0)
+    def _():
+        lower_ref[...] = jnp.zeros_like(lower_ref)
+        turn_panel(panel_ref, turned, (0, 1, last), halves, mesh_rows)
+
+    rows[:depth, :] = own_ref[...]
+    for part in range(halves):
+        rows[depth + part * size:depth + (part + 1) * size, :] = next_refs[part][...]
+        rows[2 * depth + part * size:2 * depth + (part + 1) * size, :] = prev_refs[part][...]
+    for idx in range(halves):
+        here = slice(idx * size, (idx + 1) * size)
+        for start, stop, put in ((0, 2 * depth, 0), (2 * depth, 3 * depth, last * depth)):
+            lower_ref[put:put + stop - start, here] += lax.dot_general(
+                rows[start:stop, :], side_ref[here, :], (((1,), (1,)), ((), ())), preferred_element_type=jnp.float32
+            )
+        sum_ref[here, :] = total_ref[here, :] + jnp.dot(turned[here, :], rows[...], preferred_element_type=jnp.float32)
+
+
+def late_far_kernel(halves, far_refs, panel_ref, side_ref, sum_ref, lower_ref, right_ref, turned, rows):
+    mesh_rows = panel_ref.shape[0] // halves
+    size = panel_ref.shape[2]
+
+    @pl.when(pl.program_id(0) == 0)
+    def _():
+        lower_ref[...] = jnp.zeros_like(lower_ref)
+        turn_panel(panel_ref, turned, (2,), halves, mesh_rows)
+
+    for part in range(halves):
+        rows[part * size:(part + 1) * size, :] = far_refs[part][...]
+    for idx in range(halves):
+        here = slice(idx * size, (idx + 1) * size)
+        lower_ref[:, here] += lax.dot_general(
+            rows[...], side_ref[here, :], (((1,), (1,)), ((), ())), preferred_element_type=jnp.float32
+        )
+        share = sum_ref[here, :] + jnp.dot(turned[here, :], rows[...], preferred_element_type=jnp.float32)
+        right_ref[here, :] = share.astype(right_ref.dtype)
+
+
+def run_late_near(halves, own, nexts, prevs, panel, side, total):
+    depth, size = panel.shape[1], panel.shape[2]
+    mesh_rows = panel.shape[0] // halves
+    num_cols = side.shape[1]
+    piece = min(LATE_PIECE, num_cols)
+
+    def kernel(own_ref, *refs):
+        late_near_kernel(halves, own_ref, refs[:halves], refs[halves:2 * halves], *refs[2 * halves:])
+
+    wide = pl.BlockSpec((depth, piece), lambda j: (0, j))
+    return pl.pallas_call(
+        kernel,
+        name="late_near",
+        grid=(num_cols // piece,),
+        in_specs=[wide]
+        + [pl.BlockSpec((size, piece), lambda j: (0, j))] * (2 * halves)
+        + [pl.BlockSpec(panel.shape, lambda j: (0, 0, 0)), wide, wide],
+        out_specs=[pl.BlockSpec((mesh_rows * depth, depth), lambda j: (0, 0)), wide],
+        out_shape=[
+            jax.ShapeDtypeStruct((mesh_rows * depth, depth), jnp.float32),
+            jax.ShapeDtypeStruct((depth, num_cols), jnp.float32),
+        ],
+        scratch_shapes=[pltpu.VMEM((depth, 3 * depth), jnp.bfloat16), pltpu.VMEM((3 * depth, piece), jnp.bfloat16)],
+        compiler_params=pltpu.CompilerParams(vmem_limit_bytes=56 * 1024 * 1024),
+        cost_estimate=pl.CostEstimate(flops=12 * depth * depth * num_cols, bytes_accessed=16 * depth * num_cols, transcendentals=0),
+    )(own, *nexts, *prevs, panel, side, total)
+
+
+def run_late_far(halves, fars, panel, side, total, lower, right):
+    depth, size = panel.shape[1], panel.shape[2]
+    num_cols = side.shape[1]
+    piece = min(LATE_PIECE, num_cols)
+
+    def kernel(*refs):
+        late_far_kernel(halves, refs[:halves], *refs[halves:halves + 3], *refs[halves + 5:])
+
+    wide = pl.BlockSpec((depth, piece), lambda j: (0, j))
+    anywhere = pl.BlockSpec(memory_space=pl.ANY)
+    return pl.pallas_call(
+        kernel,
+        name="late_far",
+        grid=(num_cols // piece,),
+        in_specs=[pl.BlockSpec((size, piece), lambda j: (0, j))] * halves
+        + [pl.BlockSpec(panel.shape, lambda j: (0, 0, 0)), wide, wide, anywhere, anywhere],
+        out_specs=[pl.BlockSpec((depth, depth), lambda j: (2, 0)), wide],
+        out_shape=[jax.ShapeDtypeStruct(lower.shape, jnp.float32), jax.ShapeDtypeStruct(right.shape, jnp.bfloat16)],
+        scratch_shapes=[pltpu.VMEM((depth, depth), jnp.bfloat16), pltpu.VMEM((depth, piece), jnp.bfloat16)],
+        input_output_aliases={halves + 3: 0, halves + 4: 1},
+        compiler_params=pltpu.CompilerParams(vmem_limit_bytes=56 * 1024 * 1024),
+        cost_estimate=pl.CostEstimate(flops=4 * depth * depth * num_cols, bytes_accessed=10 * depth * num_cols, transcendentals=0),
+    )(*fars, panel, side, total, lower, right)
+
+
 def solution(mesh):
     mesh_rows = mesh.shape["row"]
     mesh_cols = mesh.shape["col"]
@@ -112,7 +223,7 @@
     for row in range(mesh_rows):
         for col in range(mesh_cols):
             home, half = col % mesh_rows, col // mesh_rows
-            spread.append((row * mesh_cols + col, home * mesh_cols + half * mesh_rows + (row - home) % mesh_rows))
+            spread.append((row * mesh_cols + col, home * mesh_cols + half * mesh_rows + seat((row - home) % mesh_rows, mesh_rows)))
             rel, part = col // halves, col % halves
             for turn in range(halves):
                 owner = (row + rel) % mesh_rows * mesh_cols + row + mesh_rows * ((part + turn) % halves)
@@ -126,7 +237,10 @@
         my_half = my_col // mesh_rows
         my_part = my_col % halves
 
-        own = [grad_out[group * BLOCK_SIZE:(group + 1) * BLOCK_SIZE] for group in range(num_groups)]
+        own = {num_groups - 1: grad_out[(num_groups - 1) * BLOCK_SIZE:]}
+        own[num_groups - 1], grad_later = lax.optimization_barrier((own[num_groups - 1], grad_out))
+        for group in range(num_groups - 1):
+            own[group] = grad_later[group * BLOCK_SIZE:(group + 1) * BLOCK_SIZE]
         near = {}
         far = {}
         panels = {
@@ -194,54 +308,54 @@
                 waits += near[group - 1]
             if group + 1 in totals:
                 waits.append(totals[group + 1])
-            early = range(halves, num_groups)
-            if group == 0:
-                waits += state["sends"]
             waits = list(lax.optimization_barrier(tuple(waits)))
             blocks, panels[sup] = waits[:3], waits[3]
             waits = waits[4:]
             if group > 0:
                 near[group - 1] = (waits.pop(0), waits.pop(0))
             total = waits.pop(0) if group + 1 in totals else None
-            if group == 0:
-                state["early"] = collect_lower(waits)
             lowers[group], state["right"], *rest = run_group(
                 group, halves, [grad_out, *blocks], panels[sup], right_side, total, state["right"]
             )
             if rest:
                 totals[group] = rest[0]
-            if group in early:
-                sums[group] = lax.psum_scatter(lowers[group], "col", scatter_dimension=0, tiled=True)
-            if group == halves:
-                state["sends"] = [
-                    jnp.concatenate([widen(choose(sums[early_group], turn)) for early_group in early], axis=0)
-                    for turn in range(halves)
-                ]
+            sums[group] = lax.psum_scatter(lowers[group], "col", scatter_dimension=0, tiled=True)
 
         for sup in reversed(range(num_supers)):
             spread_panel(sup)
         send_own(num_groups - 1)
         send_own(num_groups - 2)
         forward(num_groups - 1)
-        for group in reversed(range(num_groups)):
-            if group > 0:
-                forward(group - 1)
+        for group in reversed(range(halves, num_groups)):
+            forward(group - 1)
             compute(group)
-
-        late = jnp.stack([lowers[group].reshape(mesh_rows, BLOCK_SIZE, -1) for group in range(halves)], axis=1)
-        late = lax.psum_scatter(late.reshape(rows_here * 2 * mesh_rows // num_groups, -1), "col", scatter_dimension=0, tiled=True)
-        late = by_part(collect_lower([choose(late, turn) for turn in range(halves)]))
+        for group in reversed(range(halves - 1)):
+            forward(group)
+
+        firsts = range(halves)
+        waits = lax.optimization_barrier((totals[halves], panels[0], *(block for group in firsts for block in near[group])))
+        panel, arrived = waits[1], waits[2:]
+        lower, total = run_late_near(halves, grad_out, arrived[1::2], arrived[0::2], panel, right_side, waits[0])
+        lower, total, panel, *fars = lax.optimization_barrier((lower, total, panel, *(far[group] for group in firsts)))
+        lower, grad_right = run_late_far(halves, fars, panel, right_side, total, lower, state["right"])
+        late = lax.psum_scatter(lower, "col", scatter_dimension=0, tiled=True)
+
         half_size = BLOCK_SIZE // halves
-        rest = by_part(state["early"])
-        lower_rows = [widen(piece) for piece in late]
-        for idx in range(num_groups - halves):
-            lower_rows += [piece[idx * half_size:(idx + 1) * half_size] for piece in rest]
+        lower_rows = [widen(piece) for piece in by_part(collect_lower([choose(late, turn) for turn in range(halves)]))]
+        for sup in range(1, num_supers):
+            groups = range(sup * halves, (sup + 1) * halves)
+            turns = collect_lower(
+                [jnp.concatenate([choose(sums[group], turn) for group in groups], axis=0) for turn in range(halves)],
+            )
+            pieces = by_part(turns)
+            for idx in range(halves):
+                lower_rows += [widen(piece[idx * half_size:(idx + 1) * half_size]) for piece in pieces]
         grad_lower = jnp.concatenate(lower_rows, axis=0)
         row_pos = jnp.arange(rows_here)[:, None]
         col_pos = jnp.arange(cols_here)[None, :]
         row_global = (row_pos // BLOCK_SIZE * mesh_rows + lax.axis_index("row")) * BLOCK_SIZE + row_pos % BLOCK_SIZE
         col_global = (col_pos // BLOCK_SIZE * mesh_cols + my_col) * BLOCK_SIZE + col_pos % BLOCK_SIZE
         grad_lower = jnp.where(row_global >= col_global, grad_lower, 0.0).astype(jnp.bfloat16)
-        return state["right"], grad_lower
+        return grad_right, grad_lower
 
     return jax.shard_map(shards, mesh=mesh, in_specs=(block_spec, block_spec, block_spec), out_specs=(block_spec, block_spec), check_vma=False)

time: 719 us -> 707 us (0.983)
  starting transfers between devices: 73 us -> 63.7 us
    ppermute x3, waiting for transfers between devices: 127 us -> 12.7 us  [forward(): far[group] = lax.ppermute(near[group][0], 'row', up)]
    ppermute x3, waiting for transfers between devices: 48.7 us -> 116 us  [forward(): far[group] = lax.ppermute(near[group][1], 'row', down)]
    ppermute x3, waiting for transfers between devices: 53.7 us -> 100 us  [spread_panel(): panel = lax.ppermute(panels[sup], ('row', 'col'), spread)]
    reduce_scatter x1, waiting for transfers between devices: 55 us -> 19.8 us  [shards(): late = lax.psum_scatter(lower, 'col', scatter_dimension=0, tiled=True)]
    ppermute x4 -> x6, waiting for transfers between devices: 6.5 us -> 40.7 us  [collect_lower(): lax.ppermute(send, ('row', 'col'), collect[turn])]
    pallas_call x0 -> x2, Pallas kernels: none -> 32.6 us  [the longest x1 21 us: run_late_near(): pl.pallas_call(kernel, name='late_near', grid=(num_cols // piece,), in_sp...]
    pallas_call x6 -> x4, Pallas kernels: 141 us -> 113 us  [run_group(): pl.pallas_call(functools.partial(group_kernel, group, halves, has_total),...]
    ppermute x6, waiting for transfers between devices: 98.3 us -> 80.7 us  [send_own(): lax.ppermute(own[group], 'row', up)]
  transfers between devices with their start and end apart: 33 -> 35, of which waited for: 15 -> 20; matrix products, arithmetic and copies ran while one was open for 3% -> 2% of each run, Pallas kernels for 18% -> 21%
where the time goes in v3:
time: 707 us
  waiting for transfers between devices  460 us (65%)
  Pallas kernels  145 us (21%)
  starting transfers between devices  63.7 us (9%)
  local copies, waits for them, and re-layouts  15.5 us (2%)
  between operations  14.6 us (2%)
  other arithmetic  7.75 us (1%)
    ppermute x3, waiting for transfers between devices, forward(): far[group] = lax.ppermute(near[group][1], 'row', down)  116 us
    pallas_call x4, Pallas kernels, run_group(): pl.pallas_call(functools.partial(group_kernel, group, halves, has_total),...  113 us
    ppermute x3, waiting for transfers between devices, spread_panel(): panel = lax.ppermute(panels[sup], ('row', 'col'), spread)  100 us
    ppermute x6, waiting for transfers between devices, send_own(): lax.ppermute(own[group], 'row', up)  80.7 us
    reduce_scatter x4, waiting for transfers between devices, compute(): lax.psum_scatter(lowers[group], 'col', scatter_dimension=0, tiled=True)  74.3 us
    ppermute x6, waiting for transfers between devices, collect_lower(): lax.ppermute(send, ('row', 'col'), collect[turn])  40.7 us
    ppermute x6, starting transfers between devices, collect_lower(): lax.ppermute(send, ('row', 'col'), collect[turn])  27.5 us
    pallas_call x1, Pallas kernels, run_late_near(): pl.pallas_call(kernel, name='late_near', grid=(num_cols // piece,), in_sp...  21 us
  transfers between devices with their start and end apart: 35, of which 20 were waited for; matrix products, arithmetic and copies ran while one was open for 2% of the time, Pallas kernels for 21%

profile of v3, /device:TPU:97, one launch (start us, length us, event | category | flops | bytes accessed | tf_op | source)
XLA Modules:
  0.0 706.6 jit_solution(17747252293081886256)
XLA Ops:
  7.2 1.2 slice.96
  8.4 5.7 collective-permute-start.7
  14.1 11.2 %collective-permute-done.7 = bf16[512,768]{1,0:T(8,128)(2,1)S(1)} collective-permute-done((bf16[512,768]{1,0:T(8,128)(2,1)S(1)}, bf16[512,768]{1,0:T(8,128)(2,1)S(1)}, u32[]{:S(2)}, u32[]{:S(2)}) %collective-permute-start.7) | collective-permute-done | bytes 786464 | tf_op jit(solution)/shard_map/ppermute | solution.py:259
  27.5 2.7 collective-permute-start.14
  30.2 9.3 %collective-permute-done.14 = bf16[512,512]{1,0:T(8,128)(2,1)S(1)} collective-permute-done((bf16[512,512]{1,0:T(8,128)(2,1)S(1)}, bf16[512,512]{1,0:T(8,128)(2,1)S(1)}, u32[]{:S(2)}, u32[]{:S(2)}) %collective-permute-start.14) | collective-permute-done | bytes 524320 | tf_op jit(solution)/shard_map/ppermute | solution.py:259
  40.5 1.7 slice.91
  42.8 5.4 collective-permute-start.5
  48.1 7.9 %fusion.22 = (bf16[256,4096]{1,0:T(8,128)(2,1)}, bf16[256,4096]{1,0:T(8,128)(2,1)}, bf16[256,4096]{1,0:T(8,128)(2,1)S(1)}, bf16[256,4096]{1,0:T(8,128)(2,1)}, bf16[256,4096]{1,0:T(8,128)(2,1)}) fusion(bf16[1536,4096]{1,0:T(8,128)(2,1)} %own_ref.1), kind=kLoop, calls=%fused_computation.61 | loop fusion | bytes 20971520 | tf_op jit(solution)/shard_map/slice | solution.py:243
  56.0 3.2 collective-permute-start
  59.9 34.5 %collective-permute-done.4.refs_3_ = bf16[256,4096]{1,0:T(8,128)(2,1)} collective-permute-done((bf16[256,4096]{1,0:T(8,128)(2,1)S(1)}, bf16[256,4096]{1,0:T(8,128)(2,1)}, u32[]{:S(2)}, u32[]{:S(2)}) %collective-permute-start.4) | collective-permute-done | bytes 2097184 | tf_op jit(solution)/shard_map/ppermute | solution.py:256
  94.3 3.4 collective-permute-done.5.refs_1_
  97.8 1.5 collective-permute-start.6
  100.2 2.0 collective-permute-start.18
  102.2 79.7 %collective-permute-done.18 = bf16[512,256]{1,0:T(8,128)(2,1)S(1)} collective-permute-done((bf16[512,256]{1,0:T(8,128)(2,1)S(1)}, bf16[512,256]{1,0:T(8,128)(2,1)S(1)}, u32[]{:S(2)}, u32[]{:S(2)}) %collective-permute-start.18) | collective-permute-done | bytes 262176 | tf_op jit(solution)/shard_map/ppermute | solution.py:259
  182.8 1.4 collective-permute-start.9
  184.4 2.6 collective-permute-start.3
  187.1 35.0 %shard_map.50 = (f32[1024,1536]{1,0:T(8,128)}, bf16[1536,4096]{1,0:T(8,128)(2,1)}, f32[1280,4096]{1,0:T(8,128)}) custom-call(bf16[1536,4096]{1,0:T(8,128)(2,1)} %own_ref.1, bf16[256,4096]{1,0:T(8,128)(2,1)} %copy-done.4, bf16[256,4096]{1,0:T(8,128)(2,1)} %collective-permute-done.6.refs_2_, bf16[256,4096]{1,0:T(8,128)(2,1)} %collective-permute-done.4.refs_3_, ...), custom_call_target="tpu_custom_call" | custom-call | flops 25769803776 | bytes 75497472 | tf_op jit(solution)/shard_map/pallas_call | solution.py:92
  222.1 7.9 %collective-permute-done.10.refs_1_ = bf16[256,4096]{1,0:T(8,128)(2,1)} collective-permute-done((bf16[256,4096]{1,0:T(8,128)(2,1)}, bf16[256,4096]{1,0:T(8,128)(2,1)}, u32[]{:S(2)}, u32[]{:S(2)}) %collective-permute-start.10) | collective-permute-done | bytes 2097184 | tf_op jit(solution)/shard_map/ppermute | solution.py:256
  230.0 2.1 collective-permute-done.9.refs_3_
  232.2 2.5 collective-permute-start.17
  234.8 85.1 %collective-permute-done.8.refs_2_ = bf16[256,4096]{1,0:T(8,128)(2,1)} collective-permute-done((bf16[256,4096]{1,0:T(8,128)(2,1)}, bf16[256,4096]{1,0:T(8,128)(2,1)}, u32[]{:S(2)}, u32[]{:S(2)}) %collective-permute-start.8) | collective-permute-done | bytes 2097184 | tf_op jit(solution)/shard_map/ppermute | solution.py:274
  319.9 31.3 %shard_map.51 = (f32[1024,1536]{1,0:T(8,128)}, bf16[1536,4096]{1,0:T(8,128)(2,1)}, f32[1024,4096]{1,0:T(8,128)}) custom-call(bf16[1536,4096]{1,0:T(8,128)(2,1)} %own_ref.1, bf16[256,4096]{1,0:T(8,128)(2,1)} %collective-permute-done.1.refs_1_, bf16[256,4096]{1,0:T(8,128)(2,1)} %collective-permute-done.8.refs_2_, ...), custom_call_target="tpu_custom_call", output_to_operand_aliasing={{1}: (7, {})} | custom-call | flops 21474836480 | bytes 65011712 | tf_op jit(solution)/shard_map/pallas_call | solution.py:92
  351.2 2.8 collective-permute-start.15
  354.0 10.6 %collective-permute-done.13.refs_2_ = bf16[256,4096]{1,0:T(8,128)(2,1)} collective-permute-done((bf16[256,4096]{1,0:T(8,128)(2,1)}, bf16[256,4096]{1,0:T(8,128)(2,1)}, u32[]{:S(2)}, u32[]{:S(2)}) %collective-permute-start.13) | collective-permute-done | bytes 2097184 | tf_op jit(solution)/shard_map/ppermute | solution.py:272
  364.6 25.4 %shard_map.52 = (f32[1024,1024]{1,0:T(8,128)}, bf16[1536,4096]{1,0:T(8,128)(2,1)}, f32[768,4096]{1,0:T(8,128)}) custom-call(bf16[1536,4096]{1,0:T(8,128)(2,1)} %own_ref.1, bf16[256,4096]{1,0:T(8,128)(2,1)} %collective-permute-done.10.refs_1_, bf16[256,4096]{1,0:T(8,128)(2,1)} %collective-permute-done.13.refs_2_, ...), custom_call_target="tpu_custom_call", output_to_operand_aliasing={{1}: (7, {})} | custom-call | flops 17179869184 | bytes 54525952 | tf_op jit(solution)/shard_map/pallas_call | solution.py:92
  390.0 5.6 collective-permute-done.15.refs_2_
  395.6 21.0 %shard_map.53 = (f32[1024,1024]{1,0:T(8,128)}, bf16[1536,4096]{1,0:T(8,128)(2,1)}, f32[512,4096]{1,0:T(8,128)}) custom-call(bf16[1536,4096]{1,0:T(8,128)(2,1)} %own_ref.1, bf16[256,4096]{1,0:T(8,128)(2,1)} %collective-permute-done.3.refs_1_, bf16[256,4096]{1,0:T(8,128)(2,1)} %collective-permute-done.15.refs_2_, ...), custom_call_target="tpu_custom_call", output_to_operand_aliasing={{1}: (7, {})} | custom-call | flops 12884901888 | bytes 44040192 | tf_op jit(solution)/shard_map/pallas_call | solution.py:92
  417.4 1.8 collective-permute-start.11
  420.1 44.1 %collective-permute-done.11.refs_2_ = bf16[256,4096]{1,0:T(8,128)(2,1)S(1)} collective-permute-done((bf16[256,4096]{1,0:T(8,128)(2,1)S(1)}, bf16[256,4096]{1,0:T(8,128)(2,1)S(1)}, u32[]{:S(2)}, u32[]{:S(2)}) %collective-permute-start.11) | collective-permute-done | bytes 2097184 | tf_op jit(solution)/shard_map/ppermute | solution.py:256
  464.2 2.2 collective-permute-done.12.refs_0_
  467.9 21.0 %late_near.1 = (f32[2048,512]{1,0:T(8,128)}, f32[512,4096]{1,0:T(8,128)}) custom-call(bf16[1536,4096]{1,0:T(8,128)(2,1)} %own_ref.1, bf16[256,4096]{1,0:T(8,128)(2,1)} %collective-permute-done.12.refs_0_, bf16[256,4096]{1,0:T(8,128)(2,1)} %collective-permute-done.17.refs_1_, bf16[256,4096]{1,0:T(8,128)(2,1)} %copy-done.5, ...), custom_call_target="tpu_custom_call" | custom-call | flops 12884901888 | bytes 33554432 | tf_op jit(solution)/shard_map/late_near/pallas_call | solution.py:170
  488.9 24.9 %collective-permute-done.19.refs_0_ = bf16[256,4096]{1,0:T(8,128)(2,1)S(1)} collective-permute-done((bf16[256,4096]{1,0:T(8,128)(2,1)}, bf16[256,4096]{1,0:T(8,128)(2,1)S(1)}, u32[]{:S(2)}, u32[]{:S(2)}) %collective-permute-start.19) | collective-permute-done | bytes 2097184 | tf_op jit(solution)/shard_map/ppermute | solution.py:274
  513.8 2.1 collective-permute-done.20.refs_1_
  515.9 11.5 %late_far.1 = (f32[2048,512]{1,0:T(8,128)}, bf16[1536,4096]{1,0:T(8,128)(2,1)}) custom-call(bf16[256,4096]{1,0:T(8,128)(2,1)} %copy-done, bf16[256,4096]{1,0:T(8,128)(2,1)} %collective-permute-done.20.refs_1_, bf16[8,512,256]{2,1,0:T(8,128)(2,1)} %bitcast.6, bf16[1536,4096]{1,0:T(8,128)(2,1)} %refs_3_.1, ...), custom_call_target="tpu_custom_call", output_to_operand_aliasing={{0}: (5, {}), {1}: (6, {})} | custom-call | flops 4294967296 | bytes 20971520 | tf_op jit(solution)/shard_map/late_far/pallas_call | solution.py:198
  531.4 5.5 collective-permute-start.24
  536.9 2.0 collective-permute-start.23
  539.0 23.4 %collective-permute-done.24 = bf16[256,512]{1,0:T(8,128)(2,1)S(1)} collective-permute-done((bf16[256,512]{1,0:T(8,128)(2,1)S(1)}, bf16[256,512]{1,0:T(8,128)(2,1)S(1)}, u32[]{:S(2)}, u32[]{:S(2)}) %collective-permute-start.24) | collective-permute-done | bytes 262176 | tf_op jit(solution)/shard_map/ppermute | solution.py:290
  562.5 19.8 %reduce-scatter.6.cloned.1.call-done = f32[256,512]{1,0:T(8,128)} async-done(((f32[2048,512]{1,0:T(8,128)}), f32[256,512]{1,0:T(8,128)}) %reduce-scatter.6.cloned.1.call-update) | async-done | bytes 524304 | tf_op jit(solution)/shard_map/reduce_scatter | solution.py:341
  583.3 3.7 collective-permute-start.21
  587.1 7.7 %collective-permute-start.22 = (bf16[256,256]{1,0:T(8,128)(2,1)S(1)}, bf16[256,256]{1,0:T(8,128)(2,1)S(1)}, u32[]{:S(2)}, u32[]{:S(2)}) collective-permute-start(bf16[256,256]{1,0:T(8,128)(2,1)S(1)} %get-tuple-element.171), channel_id=1, source_target_pairs={{0,0},{1,4},{2,8},{3,12},{4,16},{5,20},{6,24},{7,28},{8,9},{9,13},... | collective-permute-start | bytes 393224 | tf_op jit(solution)/shard_map/ppermute | solution.py:290
  594.7 34.1 %reduce-scatter.12.cloned.1.call-done = f32[128,1536]{1,0:T(8,128)} async-done(((f32[1024,1536]{1,0:T(8,128)}), f32[128,1536]{1,0:T(8,128)}) %reduce-scatter.12.cloned.1.call-update) | async-done | bytes 786448 | tf_op jit(solution)/shard_map/reduce_scatter | solution.py:322
  628.8 1.2 select_convert_fusion.1
  630.0 40.2 %reduce-scatter.14.cloned.1.call-done = f32[128,1536]{1,0:T(8,128)} async-done(((f32[1024,1536]{1,0:T(8,128)}), f32[128,1536]{1,0:T(8,128)}) %reduce-scatter.14.cloned.1.call-update) | async-done | bytes 786448 | tf_op jit(solution)/shard_map/reduce_scatter | solution.py:322
  671.4 3.1 collective-permute-start.25
  674.6 5.5 collective-permute-start.26
  680.3 15.3 %collective-permute-done.25 = bf16[256,768]{1,0:T(8,128)(2,1)S(1)} collective-permute-done((bf16[256,768]{1,0:T(8,128)(2,1)S(1)}, bf16[256,768]{1,0:T(8,128)(2,1)S(1)}, u32[]{:S(2)}, u32[]{:S(2)}) %collective-permute-start.25) | collective-permute-done | bytes 393248 | tf_op jit(solution)/shard_map/ppermute | solution.py:290
  695.6 2.0 collective-permute-done.26
  697.7 2.0 compare_select_fusion
  (79 shorter events, 16.3 us)
Async XLA Ops:
  7.2 179.9 %all-gather.7.cloned.1.call-start = ((), (), s32[]{:S(2)}) async-start(), calls=%async_computation.10 | async-start | bytes 7077888 | tf_op jit(solution)/shard_map/all_gather | solution.py:260
  8.4 16.9 %collective-permute-start.7 = (bf16[512,768]{1,0:T(8,128)(2,1)S(1)}, bf16[512,768]{1,0:T(8,128)(2,1)S(1)}, u32[]{:S(2)}, u32[]{:S(2)}) collective-permute-start(bf16[512,768]{1,0:T(8,128)(2,1)S(1)} %slice.96), channel_id=1, source_target_pairs={{0,0},{1,11},{2,17},{3,26},{4,4},{5,15},{6,21},{7,30},{8,2},{9,8},... | collective-permute-start | bytes 2359304 | tf_op jit(solution)/shard_map/ppermute | solution.py:259
  25.4 0.9 copy-start.1
  26.3 327.6 %all-gather.9.cloned.1.call-start = ((), (), s32[]{:S(2)}) async-start(), calls=%async_computation.11 | async-start | bytes 4718592 | tf_op jit(solution)/shard_map/all_gather | solution.py:260
  27.5 12.0 %collective-permute-start.14 = (bf16[512,512]{1,0:T(8,128)(2,1)S(1)}, bf16[512,512]{1,0:T(8,128)(2,1)S(1)}, u32[]{:S(2)}, u32[]{:S(2)}) collective-permute-start(bf16[512,512]{1,0:T(8,128)(2,1)S(1)} %slice.98), channel_id=1, source_target_pairs={{0,0},{1,11},{2,17},{3,26},{4,4},{5,15},{6,21},{7,30},{8,2},{9,8},... | collective-permute-start | bytes 1572872 | tf_op jit(solution)/shard_map/ppermute | solution.py:259
  39.5 0.8 copy-start.2
  40.4 427.5 %all-gather.11.cloned.1.call-start = ((), (), s32[]{:S(2)}) async-start(), calls=%async_computation.12 | async-start | bytes 2359296 | tf_op jit(solution)/shard_map/all_gather | solution.py:260
  42.2 52.1 %collective-permute-start.4 = (bf16[256,4096]{1,0:T(8,128)(2,1)S(1)}, bf16[256,4096]{1,0:T(8,128)(2,1)}, u32[]{:S(2)}, u32[]{:S(2)}) collective-permute-start(bf16[256,4096]{1,0:T(8,128)(2,1)S(1)} %slice.91), channel_id=1, source_target_pairs={{0,8},{8,16},{16,24},{24,0},{1,9},{9,17},{17,25},{25,1},{2,10},{10... | collective-permute-start | bytes 6291464 | tf_op jit(solution)/shard_map/ppermute | solution.py:256
  42.8 55.0 %collective-permute-start.5 = (bf16[256,4096]{1,0:T(8,128)(2,1)S(1)}, bf16[256,4096]{1,0:T(8,128)(2,1)S(1)}, u32[]{:S(2)}, u32[]{:S(2)}) collective-permute-start(bf16[256,4096]{1,0:T(8,128)(2,1)S(1)} %slice.91), channel_id=1, source_target_pairs={{0,24},{8,0},{16,8},{24,16},{1,25},{9,1},{17,9},{25,17},{2,26},{10... | collective-permute-start | bytes 6291464 | tf_op jit(solution)/shard_map/ppermute | solution.py:256
  56.0 128.3 %collective-permute-start = (bf16[256,4096]{1,0:T(8,128)(2,1)}, bf16[256,4096]{1,0:T(8,128)(2,1)}, u32[]{:S(2)}, u32[]{:S(2)}) collective-permute-start(bf16[256,4096]{1,0:T(8,128)(2,1)} %get-tuple-element.158), channel_id=1, source_target_pairs={{0,8},{8,16},{16,24},{24,0},{1,9},{9,17},{17,25},{25,1},{2,10},{10... | collective-permute-start | bytes 6291464 | tf_op jit(solution)/shard_map/ppermute | solution.py:256
  59.2 125.1 %collective-permute-start.1 = (bf16[256,4096]{1,0:T(8,128)(2,1)}, bf16[256,4096]{1,0:T(8,128)(2,1)}, u32[]{:S(2)}, u32[]{:S(2)}) collective-permute-start(bf16[256,4096]{1,0:T(8,128)(2,1)} %get-tuple-element.158), channel_id=1, source_target_pairs={{0,24},{8,0},{16,8},{24,16},{1,25},{9,1},{17,9},{25,17},{2,26},{10... | collective-permute-start | bytes 6291464 | tf_op jit(solution)/shard_map/ppermute | solution.py:256
  97.8 4.4 copy-start.4
  97.8 89.2 %collective-permute-start.6 = (bf16[256,4096]{1,0:T(8,128)(2,1)}, bf16[256,4096]{1,0:T(8,128)(2,1)}, u32[]{:S(2)}, u32[]{:S(2)}) collective-permute-start(bf16[256,4096]{1,0:T(8,128)(2,1)} %collective-permute-done.4.refs_3_), channel_id=1, source_target_pairs={{0,8},{8,16},{16,24},{24,0},{1,9},{9,17},{17,25},{25,1},{2,10},{10... | collective-permute-start | bytes 6291464 | tf_op jit(solution)/shard_map/ppermute | solution.py:272
  100.2 81.7 %collective-permute-start.18 = (bf16[512,256]{1,0:T(8,128)(2,1)S(1)}, bf16[512,256]{1,0:T(8,128)(2,1)S(1)}, u32[]{:S(2)}, u32[]{:S(2)}) collective-permute-start(bf16[512,256]{1,0:T(8,128)(2,1)S(1)} %slice.99), channel_id=1, source_target_pairs={{0,0},{1,11},{2,17},{3,26},{4,4},{5,15},{6,21},{7,30},{8,2},{9,8},... | collective-permute-start | bytes 786440 | tf_op jit(solution)/shard_map/ppermute | solution.py:259
  181.9 0.7 copy-start.3
  182.7 346.5 %reduce-scatter.8.cloned.1.call-start = ((), (), s32[]{:S(2)}) async-start(), calls=%async_computation.6 | async-start | bytes 4718592 | tf_op jit(solution)/shard_map/reduce_scatter | solution.py:322
  182.7 47.3 %collective-permute-start.10 = (bf16[256,4096]{1,0:T(8,128)(2,1)}, bf16[256,4096]{1,0:T(8,128)(2,1)}, u32[]{:S(2)}, u32[]{:S(2)}) collective-permute-start(bf16[256,4096]{1,0:T(8,128)(2,1)} %get-tuple-element.88), channel_id=1, source_target_pairs={{0,24},{8,0},{16,8},{24,16},{1,25},{9,1},{17,9},{25,17},{2,26},{10... | collective-permute-start | bytes 6291464 | tf_op jit(solution)/shard_map/ppermute | solution.py:256
  182.8 49.3 %collective-permute-start.9 = (bf16[256,4096]{1,0:T(8,128)(2,1)}, bf16[256,4096]{1,0:T(8,128)(2,1)}, u32[]{:S(2)}, u32[]{:S(2)}) collective-permute-start(bf16[256,4096]{1,0:T(8,128)(2,1)} %get-tuple-element.88), channel_id=1, source_target_pairs={{0,8},{8,16},{16,24},{24,0},{1,9},{9,17},{17,25},{25,1},{2,10},{10... | collective-permute-start | bytes 6291464 | tf_op jit(solution)/shard_map/ppermute | solution.py:256
  184.3 166.9 %collective-permute-start.2 = (bf16[256,4096]{1,0:T(8,128)(2,1)}, bf16[256,4096]{1,0:T(8,128)(2,1)}, u32[]{:S(2)}, u32[]{:S(2)}) collective-permute-start(bf16[256,4096]{1,0:T(8,128)(2,1)} %get-tuple-element.79), channel_id=1, source_target_pairs={{0,8},{8,16},{16,24},{24,0},{1,9},{9,17},{17,25},{25,1},{2,10},{10... | collective-permute-start | bytes 6291464 | tf_op jit(solution)/shard_map/ppermute | solution.py:256
  184.4 166.8 %collective-permute-start.3 = (bf16[256,4096]{1,0:T(8,128)(2,1)}, bf16[256,4096]{1,0:T(8,128)(2,1)}, u32[]{:S(2)}, u32[]{:S(2)}) collective-permute-start(bf16[256,4096]{1,0:T(8,128)(2,1)} %get-tuple-element.79), channel_id=1, source_target_pairs={{0,24},{8,0},{16,8},{24,16},{1,25},{9,1},{17,9},{25,17},{2,26},{10... | collective-permute-start | bytes 6291464 | tf_op jit(solution)/shard_map/ppermute | solution.py:256
  187.0 132.9 %collective-permute-start.8 = (bf16[256,4096]{1,0:T(8,128)(2,1)}, bf16[256,4096]{1,0:T(8,128)(2,1)}, u32[]{:S(2)}, u32[]{:S(2)}) collective-permute-start(bf16[256,4096]{1,0:T(8,128)(2,1)} %collective-permute-done.1.refs_1_), channel_id=1, source_target_pairs={{0,24},{8,0},{16,8},{24,16},{1,25},{9,1},{17,9},{25,17},{2,26},{10... | collective-permute-start | bytes 6291464 | tf_op jit(solution)/shard_map/ppermute | solution.py:274
  232.1 157.9 %collective-permute-start.16 = (bf16[256,4096]{1,0:T(8,128)(2,1)}, bf16[256,4096]{1,0:T(8,128)(2,1)}, u32[]{:S(2)}, u32[]{:S(2)}) collective-permute-start(bf16[256,4096]{1,0:T(8,128)(2,1)} %get-tuple-element.112), channel_id=1, source_target_pairs={{0,8},{8,16},{16,24},{24,0},{1,9},{9,17},{17,25},{25,1},{2,10},{10... | collective-permute-start | bytes 6291464 | tf_op jit(solution)/shard_map/ppermute | solution.py:256
  232.2 157.8 %collective-permute-start.17 = (bf16[256,4096]{1,0:T(8,128)(2,1)}, bf16[256,4096]{1,0:T(8,128)(2,1)}, u32[]{:S(2)}, u32[]{:S(2)}) collective-permute-start(bf16[256,4096]{1,0:T(8,128)(2,1)} %get-tuple-element.112), channel_id=1, source_target_pairs={{0,24},{8,0},{16,8},{24,16},{1,25},{9,1},{17,9},{25,17},{2,26},{10... | collective-permute-start | bytes 6291464 | tf_op jit(solution)/shard_map/ppermute | solution.py:256
  319.9 44.7 %collective-permute-start.13 = (bf16[256,4096]{1,0:T(8,128)(2,1)}, bf16[256,4096]{1,0:T(8,128)(2,1)}, u32[]{:S(2)}, u32[]{:S(2)}) collective-permute-start(bf16[256,4096]{1,0:T(8,128)(2,1)} %collective-permute-done.9.refs_3_), channel_id=1, source_target_pairs={{0,8},{8,16},{16,24},{24,0},{1,9},{9,17},{17,25},{25,1},{2,10},{10... | collective-permute-start | bytes 6291464 | tf_op jit(solution)/shard_map/ppermute | solution.py:272
  351.2 44.4 %collective-permute-start.15 = (bf16[256,4096]{1,0:T(8,128)(2,1)}, bf16[256,4096]{1,0:T(8,128)(2,1)}, u32[]{:S(2)}, u32[]{:S(2)}) collective-permute-start(bf16[256,4096]{1,0:T(8,128)(2,1)} %collective-permute-done.3.refs_1_), channel_id=1, source_target_pairs={{0,24},{8,0},{16,8},{24,16},{1,25},{9,1},{17,9},{25,17},{2,26},{10... | collective-permute-start | bytes 6291464 | tf_op jit(solution)/shard_map/ppermute | solution.py:274
  416.6 113.6 %reduce-scatter.10.cloned.1.call-start = ((), (), s32[]{:S(2)}) async-start(), calls=%async_computation.7 | async-start | bytes 4718592 | tf_op jit(solution)/shard_map/reduce_scatter | solution.py:322
  417.3 164.9 %reduce-scatter.6.cloned.1.call-start = ((), (), s32[]{:S(2)}) async-start(), calls=%async_computation.5 | async-start | bytes 4718592 | tf_op jit(solution)/shard_map/reduce_scatter | solution.py:341
  417.4 46.9 %collective-permute-start.11 = (bf16[256,4096]{1,0:T(8,128)(2,1)S(1)}, bf16[256,4096]{1,0:T(8,128)(2,1)S(1)}, u32[]{:S(2)}, u32[]{:S(2)}) collective-permute-start(bf16[256,4096]{1,0:T(8,128)(2,1)S(1)} %get-tuple-element.103), channel_id=1, source_target_pairs={{0,8},{8,16},{16,24},{24,0},{1,9},{9,17},{17,25},{25,1},{2,10},{10... | collective-permute-start | bytes 6291464 | tf_op jit(solution)/shard_map/ppermute | solution.py:256
  419.2 47.3 %collective-permute-start.12 = (bf16[256,4096]{1,0:T(8,128)(2,1)S(1)}, bf16[256,4096]{1,0:T(8,128)(2,1)}, u32[]{:S(2)}, u32[]{:S(2)}) collective-permute-start(bf16[256,4096]{1,0:T(8,128)(2,1)S(1)} %get-tuple-element.103), channel_id=1, source_target_pairs={{0,24},{8,0},{16,8},{24,16},{1,25},{9,1},{17,9},{25,17},{2,26},{10... | collective-permute-start | bytes 6291464 | tf_op jit(solution)/shard_map/ppermute | solution.py:256
  464.2 2.2 copy-start.5
  466.4 47.4 %collective-permute-start.19 = (bf16[256,4096]{1,0:T(8,128)(2,1)}, bf16[256,4096]{1,0:T(8,128)(2,1)S(1)}, u32[]{:S(2)}, u32[]{:S(2)}) collective-permute-start(bf16[256,4096]{1,0:T(8,128)(2,1)} %collective-permute-done.12.refs_0_), channel_id=1, source_target_pairs={{0,24},{8,0},{16,8},{24,16},{1,25},{9,1},{17,9},{25,17},{2,26},{10... | collective-permute-start | bytes 6291464 | tf_op jit(solution)/shard_map/ppermute | solution.py:274
  467.5 48.4 %collective-permute-start.20 = (bf16[256,4096]{1,0:T(8,128)(2,1)}, bf16[256,4096]{1,0:T(8,128)(2,1)}, u32[]{:S(2)}, u32[]{:S(2)}) collective-permute-start(bf16[256,4096]{1,0:T(8,128)(2,1)} %collective-permute-done.16.refs_3_), channel_id=1, source_target_pairs={{0,8},{8,16},{16,24},{24,0},{1,9},{9,17},{17,25},{25,1},{2,10},{10... | collective-permute-start | bytes 6291464 | tf_op jit(solution)/shard_map/ppermute | solution.py:272
  513.8 2.1 copy-start
  527.5 101.3 %reduce-scatter.12.cloned.1.call-start = ((), (), s32[]{:S(2)}) async-start(), calls=%async_computation.8 | async-start | bytes 7077888 | tf_op jit(solution)/shard_map/reduce_scatter | solution.py:322
  528.3 141.8 %reduce-scatter.14.cloned.1.call-start = ((), (), s32[]{:S(2)}) async-start(), calls=%async_computation.9 | async-start | bytes 7077888 | tf_op jit(solution)/shard_map/reduce_scatter | solution.py:322
  531.4 31.0 %collective-permute-start.24 = (bf16[256,512]{1,0:T(8,128)(2,1)S(1)}, bf16[256,512]{1,0:T(8,128)(2,1)S(1)}, u32[]{:S(2)}, u32[]{:S(2)}) collective-permute-start(bf16[256,512]{1,0:T(8,128)(2,1)S(1)} %pad_maximum_fusion.3), channel_id=1, source_target_pairs={{0,0},{1,4},{2,8},{3,12},{4,16},{5,20},{6,24},{7,28},{8,9},{9,13},... | collective-permute-start | bytes 786440 | tf_op jit(solution)/shard_map/ppermute | solution.py:290
  536.9 25.4 %collective-permute-start.23 = (bf16[256,512]{1,0:T(8,128)(2,1)S(1)}, bf16[256,512]{1,0:T(8,128)(2,1)S(1)}, u32[]{:S(2)}, u32[]{:S(2)}) collective-permute-start(bf16[256,512]{1,0:T(8,128)(2,1)S(1)} %pad_maximum_fusion.2), channel_id=1, source_target_pairs={{0,4},{1,0},{2,12},{3,8},{4,20},{5,16},{6,28},{7,24},{8,13},{9,9},... | collective-permute-start | bytes 786440 | tf_op jit(solution)/shard_map/ppermute | solution.py:290
  583.3 96.8 %collective-permute-start.21 = (bf16[256,256]{1,0:T(8,128)(2,1)S(1)}, bf16[256,256]{1,0:T(8,128)(2,1)S(1)}, u32[]{:S(2)}, u32[]{:S(2)}) collective-permute-start(bf16[256,256]{1,0:T(8,128)(2,1)S(1)} %get-tuple-element.172), channel_id=1, source_target_pairs={{0,4},{1,0},{2,12},{3,8},{4,20},{5,16},{6,28},{7,24},{8,13},{9,9},... | collective-permute-start | bytes 393224 | tf_op jit(solution)/shard_map/ppermute | solution.py:290
  587.1 93.0 %collective-permute-start.22 = (bf16[256,256]{1,0:T(8,128)(2,1)S(1)}, bf16[256,256]{1,0:T(8,128)(2,1)S(1)}, u32[]{:S(2)}, u32[]{:S(2)}) collective-permute-start(bf16[256,256]{1,0:T(8,128)(2,1)S(1)} %get-tuple-element.171), channel_id=1, source_target_pairs={{0,0},{1,4},{2,8},{3,12},{4,16},{5,20},{6,24},{7,28},{8,9},{9,13},... | collective-permute-start | bytes 393224 | tf_op jit(solution)/shard_map/ppermute | solution.py:290
  671.4 24.2 %collective-permute-start.25 = (bf16[256,768]{1,0:T(8,128)(2,1)S(1)}, bf16[256,768]{1,0:T(8,128)(2,1)S(1)}, u32[]{:S(2)}, u32[]{:S(2)}) collective-permute-start(bf16[256,768]{1,0:T(8,128)(2,1)S(1)} %pad_maximum_fusion), channel_id=1, source_target_pairs={{0,4},{1,0},{2,12},{3,8},{4,20},{5,16},{6,28},{7,24},{8,13},{9,9},... | collective-permute-start | bytes 1179656 | tf_op jit(solution)/shard_map/ppermute | solution.py:290
  674.6 23.0 %collective-permute-start.26 = (bf16[256,768]{1,0:T(8,128)(2,1)S(1)}, bf16[256,768]{1,0:T(8,128)(2,1)S(1)}, u32[]{:S(2)}, u32[]{:S(2)}) collective-permute-start(bf16[256,768]{1,0:T(8,128)(2,1)S(1)} %pad_maximum_fusion.1), channel_id=1, source_target_pairs={{0,0},{1,4},{2,8},{3,12},{4,16},{5,20},{6,24},{7,28},{8,9},{9,13},... | collective-permute-start | bytes 1179656 | tf_op jit(solution)/shard_map/ppermute | solution.py:290
Sparse Core Ops, SparseCore 0:
  26.4 42.1 all-gather.6
  70.3 28.5 all-gather.8
  182.8 24.1 all-gather.10
  416.8 47.2 reduce-scatter.7
  466.3 34.8 reduce-scatter.9
  527.6 54.5 reduce-scatter.5
  584.6 44.2 reduce-scatter.11
  631.1 38.9 reduce-scatter.13

commit v4 on v3

--- a/solution.py
+++ b/solution.py
@@ -340,14 +340,17 @@
         lower, grad_right = run_late_far(halves, fars, panel, right_side, total, lower, state["right"])
         late = lax.psum_scatter(lower, "col", scatter_dimension=0, tiled=True)
 
+        turns = []
+        for sup in range(1, num_supers):
+            groups = range(sup * halves, (sup + 1) * halves)
+            turns += collect_lower(
+                [jnp.concatenate([choose(sums[group], turn) for group in groups], axis=0) for turn in range(halves)],
+            )
+        late, *turns = lax.optimization_barrier((late, *turns))
         half_size = BLOCK_SIZE // halves
         lower_rows = [widen(piece) for piece in by_part(collect_lower([choose(late, turn) for turn in range(halves)]))]
         for sup in range(1, num_supers):
-            groups = range(sup * halves, (sup + 1) * halves)
-            turns = collect_lower(
-                [jnp.concatenate([choose(sums[group], turn) for group in groups], axis=0) for turn in range(halves)],
-            )
-            pieces = by_part(turns)
+            pieces = by_part(turns[(sup - 1) * halves:sup * halves])
             for idx in range(halves):
                 lower_rows += [widen(piece[idx * half_size:(idx + 1) * half_size]) for piece in pieces]
         grad_lower = jnp.concatenate(lower_rows, axis=0)

time: 707 us -> 672 us (0.950)
  waiting for transfers between devices: 460 us -> 426 us
    reduce_scatter x4, waiting for transfers between devices: 74.3 us -> 53.8 us  [compute(): lax.psum_scatter(lowers[group], 'col', scatter_dimension=0, tiled=True)]
    ppermute x6, waiting for transfers between devices: 40.7 us -> 30.2 us  [collect_lower(): lax.ppermute(send, ('row', 'col'), collect[turn])]
  transfers between devices with their start and end apart: 35 -> 35, of which waited for: 20 -> 20; matrix products, arithmetic and copies ran while one was open for 2% -> 2% of each run, Pallas kernels for 21% -> 22%
where the time goes in v4:
time: 672 us; the launch traced here: 671 us
  waiting for transfers between devices  426 us (63%)
  Pallas kernels  146 us (22%)
  starting transfers between devices  62 us (9%)
  local copies, waits for them, and re-layouts  15.5 us (2%)
  between operations  14.6 us (2%)
  other arithmetic  7.78 us (1%)
    ppermute x3, waiting for transfers between devices, forward(): far[group] = lax.ppermute(near[group][1], 'row', down)  115 us
    pallas_call x4, Pallas kernels, run_group(): pl.pallas_call(functools.partial(group_kernel, group, halves, has_total),...  113 us
    ppermute x3, waiting for transfers between devices, spread_panel(): panel = lax.ppermute(panels[sup], ('row', 'col'), spread)  100 us
    ppermute x6, waiting for transfers between devices, send_own(): lax.ppermute(own[group], 'row', up)  80.7 us
    reduce_scatter x4, waiting for transfers between devices, compute(): lax.psum_scatter(lowers[group], 'col', scatter_dimension=0, tiled=True)  53.8 us
    ppermute x6, waiting for transfers between devices, collect_lower(): lax.ppermute(send, ('row', 'col'), collect[turn])  30.2 us
    ppermute x6, starting transfers between devices, collect_lower(): lax.ppermute(send, ('row', 'col'), collect[turn])  25.9 us
    pallas_call x1, Pallas kernels, run_late_near(): pl.pallas_call(kernel, name='late_near', grid=(num_cols // piece,), in_sp...  21 us
  transfers between devices with their start and end apart: 35, of which 20 were waited for; matrix products, arithmetic and copies ran while one was open for 2% of the time, Pallas kernels for 22%

profile of v4, /device:TPU:97, one launch (start us, length us, event | category | flops | bytes accessed | tf_op | source)
XLA Modules:
  0.0 671.2 jit_solution(6977529814162103582)
XLA Ops:
  7.2 1.2 slice.96
  8.4 5.7 collective-permute-start.7
  14.1 11.2 %collective-permute-done.7 = bf16[512,768]{1,0:T(8,128)(2,1)S(1)} collective-permute-done((bf16[512,768]{1,0:T(8,128)(2,1)S(1)}, bf16[512,768]{1,0:T(8,128)(2,1)S(1)}, u32[]{:S(2)}, u32[]{:S(2)}) %collective-permute-start.7) | collective-permute-done | bytes 786464 | tf_op jit(solution)/shard_map/ppermute | solution.py:259
  27.5 2.7 collective-permute-start.14
  30.2 9.3 %collective-permute-done.14 = bf16[512,512]{1,0:T(8,128)(2,1)S(1)} collective-permute-done((bf16[512,512]{1,0:T(8,128)(2,1)S(1)}, bf16[512,512]{1,0:T(8,128)(2,1)S(1)}, u32[]{:S(2)}, u32[]{:S(2)}) %collective-permute-start.14) | collective-permute-done | bytes 524320 | tf_op jit(solution)/shard_map/ppermute | solution.py:259
  40.5 1.7 slice.91
  42.8 5.4 collective-permute-start.5
  48.1 7.9 %fusion.22 = (bf16[256,4096]{1,0:T(8,128)(2,1)}, bf16[256,4096]{1,0:T(8,128)(2,1)}, bf16[256,4096]{1,0:T(8,128)(2,1)S(1)}, bf16[256,4096]{1,0:T(8,128)(2,1)}, bf16[256,4096]{1,0:T(8,128)(2,1)}) fusion(bf16[1536,4096]{1,0:T(8,128)(2,1)} %own_ref.1), kind=kLoop, calls=%fused_computation.61 | loop fusion | bytes 20971520 | tf_op jit(solution)/shard_map/slice | solution.py:243
  56.0 3.2 collective-permute-start
  59.9 34.5 %collective-permute-done.4.refs_3_ = bf16[256,4096]{1,0:T(8,128)(2,1)} collective-permute-done((bf16[256,4096]{1,0:T(8,128)(2,1)S(1)}, bf16[256,4096]{1,0:T(8,128)(2,1)}, u32[]{:S(2)}, u32[]{:S(2)}) %collective-permute-start.4) | collective-permute-done | bytes 2097184 | tf_op jit(solution)/shard_map/ppermute | solution.py:256
  94.3 3.4 collective-permute-done.5.refs_1_
  97.8 1.5 collective-permute-start.6
  100.2 2.0 collective-permute-start.18
  102.2 79.7 %collective-permute-done.18 = bf16[512,256]{1,0:T(8,128)(2,1)S(1)} collective-permute-done((bf16[512,256]{1,0:T(8,128)(2,1)S(1)}, bf16[512,256]{1,0:T(8,128)(2,1)S(1)}, u32[]{:S(2)}, u32[]{:S(2)}) %collective-permute-start.18) | collective-permute-done | bytes 262176 | tf_op jit(solution)/shard_map/ppermute | solution.py:259
  182.8 1.4 collective-permute-start.9
  184.4 2.6 collective-permute-start.3
  187.1 35.0 %shard_map.50 = (f32[1024,1536]{1,0:T(8,128)}, bf16[1536,4096]{1,0:T(8,128)(2,1)}, f32[1280,4096]{1,0:T(8,128)}) custom-call(bf16[1536,4096]{1,0:T(8,128)(2,1)} %own_ref.1, bf16[256,4096]{1,0:T(8,128)(2,1)} %copy-done.4, bf16[256,4096]{1,0:T(8,128)(2,1)} %collective-permute-done.6.refs_2_, bf16[256,4096]{1,0:T(8,128)(2,1)} %collective-permute-done.4.refs_3_, ...), custom_call_target="tpu_custom_call" | custom-call | flops 25769803776 | bytes 75497472 | tf_op jit(solution)/shard_map/pallas_call | solution.py:92
  222.1 7.9 %collective-permute-done.10.refs_1_ = bf16[256,4096]{1,0:T(8,128)(2,1)} collective-permute-done((bf16[256,4096]{1,0:T(8,128)(2,1)}, bf16[256,4096]{1,0:T(8,128)(2,1)}, u32[]{:S(2)}, u32[]{:S(2)}) %collective-permute-start.10) | collective-permute-done | bytes 2097184 | tf_op jit(solution)/shard_map/ppermute | solution.py:256
  230.0 2.1 collective-permute-done.9.refs_3_
  232.2 2.5 collective-permute-start.17
  234.8 85.1 %collective-permute-done.8.refs_2_ = bf16[256,4096]{1,0:T(8,128)(2,1)} collective-permute-done((bf16[256,4096]{1,0:T(8,128)(2,1)}, bf16[256,4096]{1,0:T(8,128)(2,1)}, u32[]{:S(2)}, u32[]{:S(2)}) %collective-permute-start.8) | collective-permute-done | bytes 2097184 | tf_op jit(solution)/shard_map/ppermute | solution.py:274
  319.9 31.3 %shard_map.51 = (f32[1024,1536]{1,0:T(8,128)}, bf16[1536,4096]{1,0:T(8,128)(2,1)}, f32[1024,4096]{1,0:T(8,128)}) custom-call(bf16[1536,4096]{1,0:T(8,128)(2,1)} %own_ref.1, bf16[256,4096]{1,0:T(8,128)(2,1)} %collective-permute-done.1.refs_1_, bf16[256,4096]{1,0:T(8,128)(2,1)} %collective-permute-done.8.refs_2_, ...), custom_call_target="tpu_custom_call", output_to_operand_aliasing={{1}: (7, {})} | custom-call | flops 21474836480 | bytes 65011712 | tf_op jit(solution)/shard_map/pallas_call | solution.py:92
  351.2 2.8 collective-permute-start.15
  354.0 10.6 %collective-permute-done.13.refs_2_ = bf16[256,4096]{1,0:T(8,128)(2,1)} collective-permute-done((bf16[256,4096]{1,0:T(8,128)(2,1)}, bf16[256,4096]{1,0:T(8,128)(2,1)}, u32[]{:S(2)}, u32[]{:S(2)}) %collective-permute-start.13) | collective-permute-done | bytes 2097184 | tf_op jit(solution)/shard_map/ppermute | solution.py:272
  364.6 25.4 %shard_map.52 = (f32[1024,1024]{1,0:T(8,128)}, bf16[1536,4096]{1,0:T(8,128)(2,1)}, f32[768,4096]{1,0:T(8,128)}) custom-call(bf16[1536,4096]{1,0:T(8,128)(2,1)} %own_ref.1, bf16[256,4096]{1,0:T(8,128)(2,1)} %collective-permute-done.10.refs_1_, bf16[256,4096]{1,0:T(8,128)(2,1)} %collective-permute-done.13.refs_2_, ...), custom_call_target="tpu_custom_call", output_to_operand_aliasing={{1}: (7, {})} | custom-call | flops 17179869184 | bytes 54525952 | tf_op jit(solution)/shard_map/pallas_call | solution.py:92
  390.0 5.6 collective-permute-done.15.refs_2_
  395.6 21.0 %shard_map.53 = (f32[1024,1024]{1,0:T(8,128)}, bf16[1536,4096]{1,0:T(8,128)(2,1)}, f32[512,4096]{1,0:T(8,128)}) custom-call(bf16[1536,4096]{1,0:T(8,128)(2,1)} %own_ref.1, bf16[256,4096]{1,0:T(8,128)(2,1)} %collective-permute-done.3.refs_1_, bf16[256,4096]{1,0:T(8,128)(2,1)} %collective-permute-done.15.refs_2_, ...), custom_call_target="tpu_custom_call", output_to_operand_aliasing={{1}: (7, {})} | custom-call | flops 12884901888 | bytes 44040192 | tf_op jit(solution)/shard_map/pallas_call | solution.py:92
  418.8 1.8 collective-permute-start.11
  421.6 44.1 %collective-permute-done.11.refs_2_ = bf16[256,4096]{1,0:T(8,128)(2,1)S(1)} collective-permute-done((bf16[256,4096]{1,0:T(8,128)(2,1)S(1)}, bf16[256,4096]{1,0:T(8,128)(2,1)S(1)}, u32[]{:S(2)}, u32[]{:S(2)}) %collective-permute-start.11) | collective-permute-done | bytes 2097184 | tf_op jit(solution)/shard_map/ppermute | solution.py:256
  465.7 2.0 collective-permute-done.12.refs_0_
  467.7 1.2 collective-permute-start.19
  469.2 21.0 %late_near.1 = (f32[2048,512]{1,0:T(8,128)}, f32[512,4096]{1,0:T(8,128)}) custom-call(bf16[1536,4096]{1,0:T(8,128)(2,1)} %own_ref.1, bf16[256,4096]{1,0:T(8,128)(2,1)} %collective-permute-done.12.refs_0_, bf16[256,4096]{1,0:T(8,128)(2,1)} %collective-permute-done.17.refs_1_, bf16[256,4096]{1,0:T(8,128)(2,1)} %copy-done.5, ...), custom_call_target="tpu_custom_call" | custom-call | flops 12884901888 | bytes 33554432 | tf_op jit(solution)/shard_map/late_near/pallas_call | solution.py:170
  490.2 24.7 %collective-permute-done.19.refs_0_ = bf16[256,4096]{1,0:T(8,128)(2,1)S(1)} collective-permute-done((bf16[256,4096]{1,0:T(8,128)(2,1)}, bf16[256,4096]{1,0:T(8,128)(2,1)S(1)}, u32[]{:S(2)}, u32[]{:S(2)}) %collective-permute-start.19) | collective-permute-done | bytes 2097184 | tf_op jit(solution)/shard_map/ppermute | solution.py:274
  514.9 2.7 collective-permute-done.20.refs_1_
  517.7 11.9 %late_far.1 = (f32[2048,512]{1,0:T(8,128)}, bf16[1536,4096]{1,0:T(8,128)(2,1)}) custom-call(bf16[256,4096]{1,0:T(8,128)(2,1)} %copy-done, bf16[256,4096]{1,0:T(8,128)(2,1)} %collective-permute-done.20.refs_1_, bf16[8,512,256]{2,1,0:T(8,128)(2,1)} %bitcast.6, bf16[1536,4096]{1,0:T(8,128)(2,1)} %refs_3_.1, ...), custom_call_target="tpu_custom_call", output_to_operand_aliasing={{0}: (5, {}), {1}: (6, {})} | custom-call | flops 4294967296 | bytes 20971520 | tf_op jit(solution)/shard_map/late_far/pallas_call | solution.py:198
  531.8 12.9 %reduce-scatter.12.cloned.1.call-done = f32[128,1536]{1,0:T(8,128)} async-done(((f32[1024,1536]{1,0:T(8,128)}), f32[128,1536]{1,0:T(8,128)}) %reduce-scatter.12.cloned.1.call-update) | async-done | bytes 786448 | tf_op jit(solution)/shard_map/reduce_scatter | solution.py:322
  544.7 1.2 select_convert_fusion.1
  545.9 40.8 %reduce-scatter.14.cloned.1.call-done = f32[128,1536]{1,0:T(8,128)} async-done(((f32[1024,1536]{1,0:T(8,128)}), f32[128,1536]{1,0:T(8,128)}) %reduce-scatter.14.cloned.1.call-update) | async-done | bytes 786448 | tf_op jit(solution)/shard_map/reduce_scatter | solution.py:322
  587.9 3.7 collective-permute-start.23
  591.6 2.0 collective-permute-start.24
  593.6 7.4 %collective-permute-start.22 = (bf16[256,512]{1,0:T(8,128)(2,1)S(1)}, bf16[256,512]{1,0:T(8,128)(2,1)S(1)}, u32[]{:S(2)}, u32[]{:S(2)}) collective-permute-start(bf16[256,512]{1,0:T(8,128)(2,1)S(1)} %pad_maximum_fusion.3), channel_id=1, source_target_pairs={{0,4},{1,0},{2,12},{3,8},{4,20},{5,16},{6,28},{7,24},{8,13},{9,9},... | collective-permute-start | bytes 786440 | tf_op jit(solution)/shard_map/ppermute | solution.py:290
  601.1 5.4 collective-permute-start.21
  606.6 23.9 %collective-permute-done.22 = bf16[256,512]{1,0:T(8,128)(2,1)S(1)} collective-permute-done((bf16[256,512]{1,0:T(8,128)(2,1)S(1)}, bf16[256,512]{1,0:T(8,128)(2,1)S(1)}, u32[]{:S(2)}, u32[]{:S(2)}) %collective-permute-start.22) | collective-permute-done | bytes 262176 | tf_op jit(solution)/shard_map/ppermute | solution.py:290
  630.4 16.6 %reduce-scatter.6.cloned.1.call-done = f32[256,512]{1,0:T(8,128)} async-done(((f32[2048,512]{1,0:T(8,128)}), f32[256,512]{1,0:T(8,128)}) %reduce-scatter.6.cloned.1.call-update) | async-done | bytes 524304 | tf_op jit(solution)/shard_map/reduce_scatter | solution.py:341
  648.1 5.5 collective-permute-start.25
  653.6 2.0 collective-permute-start.26
  656.7 5.3 collective-permute-done.26
  662.3 2.0 compare_select_fusion
  (79 shorter events, 15.9 us)
Async XLA Ops:
  7.2 179.9 %all-gather.7.cloned.1.call-start = ((), (), s32[]{:S(2)}) async-start(), calls=%async_computation.10 | async-start | bytes 7077888 | tf_op jit(solution)/shard_map/all_gather | solution.py:260
  8.4 16.9 %collective-permute-start.7 = (bf16[512,768]{1,0:T(8,128)(2,1)S(1)}, bf16[512,768]{1,0:T(8,128)(2,1)S(1)}, u32[]{:S(2)}, u32[]{:S(2)}) collective-permute-start(bf16[512,768]{1,0:T(8,128)(2,1)S(1)} %slice.96), channel_id=1, source_target_pairs={{0,0},{1,11},{2,17},{3,26},{4,4},{5,15},{6,21},{7,30},{8,2},{9,8},... | collective-permute-start | bytes 2359304 | tf_op jit(solution)/shard_map/ppermute | solution.py:259
  25.4 0.9 copy-start.1
  26.3 327.6 %all-gather.9.cloned.1.call-start = ((), (), s32[]{:S(2)}) async-start(), calls=%async_computation.11 | async-start | bytes 4718592 | tf_op jit(solution)/shard_map/all_gather | solution.py:260
  27.5 12.0 %collective-permute-start.14 = (bf16[512,512]{1,0:T(8,128)(2,1)S(1)}, bf16[512,512]{1,0:T(8,128)(2,1)S(1)}, u32[]{:S(2)}, u32[]{:S(2)}) collective-permute-start(bf16[512,512]{1,0:T(8,128)(2,1)S(1)} %slice.98), channel_id=1, source_target_pairs={{0,0},{1,11},{2,17},{3,26},{4,4},{5,15},{6,21},{7,30},{8,2},{9,8},... | collective-permute-start | bytes 1572872 | tf_op jit(solution)/shard_map/ppermute | solution.py:259
  39.5 0.8 copy-start.2
  40.4 428.8 %all-gather.11.cloned.1.call-start = ((), (), s32[]{:S(2)}) async-start(), calls=%async_computation.12 | async-start | bytes 2359296 | tf_op jit(solution)/shard_map/all_gather | solution.py:260
  42.2 52.1 %collective-permute-start.4 = (bf16[256,4096]{1,0:T(8,128)(2,1)S(1)}, bf16[256,4096]{1,0:T(8,128)(2,1)}, u32[]{:S(2)}, u32[]{:S(2)}) collective-permute-start(bf16[256,4096]{1,0:T(8,128)(2,1)S(1)} %slice.91), channel_id=1, source_target_pairs={{0,8},{8,16},{16,24},{24,0},{1,9},{9,17},{17,25},{25,1},{2,10},{10... | collective-permute-start | bytes 6291464 | tf_op jit(solution)/shard_map/ppermute | solution.py:256
  42.8 55.0 %collective-permute-start.5 = (bf16[256,4096]{1,0:T(8,128)(2,1)S(1)}, bf16[256,4096]{1,0:T(8,128)(2,1)S(1)}, u32[]{:S(2)}, u32[]{:S(2)}) collective-permute-start(bf16[256,4096]{1,0:T(8,128)(2,1)S(1)} %slice.91), channel_id=1, source_target_pairs={{0,24},{8,0},{16,8},{24,16},{1,25},{9,1},{17,9},{25,17},{2,26},{10... | collective-permute-start | bytes 6291464 | tf_op jit(solution)/shard_map/ppermute | solution.py:256
  56.0 128.3 %collective-permute-start = (bf16[256,4096]{1,0:T(8,128)(2,1)}, bf16[256,4096]{1,0:T(8,128)(2,1)}, u32[]{:S(2)}, u32[]{:S(2)}) collective-permute-start(bf16[256,4096]{1,0:T(8,128)(2,1)} %get-tuple-element.168), channel_id=1, source_target_pairs={{0,8},{8,16},{16,24},{24,0},{1,9},{9,17},{17,25},{25,1},{2,10},{10... | collective-permute-start | bytes 6291464 | tf_op jit(solution)/shard_map/ppermute | solution.py:256
  59.2 125.1 %collective-permute-start.1 = (bf16[256,4096]{1,0:T(8,128)(2,1)}, bf16[256,4096]{1,0:T(8,128)(2,1)}, u32[]{:S(2)}, u32[]{:S(2)}) collective-permute-start(bf16[256,4096]{1,0:T(8,128)(2,1)} %get-tuple-element.168), channel_id=1, source_target_pairs={{0,24},{8,0},{16,8},{24,16},{1,25},{9,1},{17,9},{25,17},{2,26},{10... | collective-permute-start | bytes 6291464 | tf_op jit(solution)/shard_map/ppermute | solution.py:256
  97.8 4.4 copy-start.4
  97.8 89.2 %collective-permute-start.6 = (bf16[256,4096]{1,0:T(8,128)(2,1)}, bf16[256,4096]{1,0:T(8,128)(2,1)}, u32[]{:S(2)}, u32[]{:S(2)}) collective-permute-start(bf16[256,4096]{1,0:T(8,128)(2,1)} %collective-permute-done.4.refs_3_), channel_id=1, source_target_pairs={{0,8},{8,16},{16,24},{24,0},{1,9},{9,17},{17,25},{25,1},{2,10},{10... | collective-permute-start | bytes 6291464 | tf_op jit(solution)/shard_map/ppermute | solution.py:272
  100.2 81.7 %collective-permute-start.18 = (bf16[512,256]{1,0:T(8,128)(2,1)S(1)}, bf16[512,256]{1,0:T(8,128)(2,1)S(1)}, u32[]{:S(2)}, u32[]{:S(2)}) collective-permute-start(bf16[512,256]{1,0:T(8,128)(2,1)S(1)} %slice.99), channel_id=1, source_target_pairs={{0,0},{1,11},{2,17},{3,26},{4,4},{5,15},{6,21},{7,30},{8,2},{9,8},... | collective-permute-start | bytes 786440 | tf_op jit(solution)/shard_map/ppermute | solution.py:259
  181.9 0.7 copy-start.3
  182.7 347.0 %reduce-scatter.8.cloned.1.call-start = ((), (), s32[]{:S(2)}) async-start(), calls=%async_computation.6 | async-start | bytes 4718592 | tf_op jit(solution)/shard_map/reduce_scatter | solution.py:322
  182.7 47.3 %collective-permute-start.10 = (bf16[256,4096]{1,0:T(8,128)(2,1)}, bf16[256,4096]{1,0:T(8,128)(2,1)}, u32[]{:S(2)}, u32[]{:S(2)}) collective-permute-start(bf16[256,4096]{1,0:T(8,128)(2,1)} %get-tuple-element.93), channel_id=1, source_target_pairs={{0,24},{8,0},{16,8},{24,16},{1,25},{9,1},{17,9},{25,17},{2,26},{10... | collective-permute-start | bytes 6291464 | tf_op jit(solution)/shard_map/ppermute | solution.py:256
  182.8 49.3 %collective-permute-start.9 = (bf16[256,4096]{1,0:T(8,128)(2,1)}, bf16[256,4096]{1,0:T(8,128)(2,1)}, u32[]{:S(2)}, u32[]{:S(2)}) collective-permute-start(bf16[256,4096]{1,0:T(8,128)(2,1)} %get-tuple-element.93), channel_id=1, source_target_pairs={{0,8},{8,16},{16,24},{24,0},{1,9},{9,17},{17,25},{25,1},{2,10},{10... | collective-permute-start | bytes 6291464 | tf_op jit(solution)/shard_map/ppermute | solution.py:256
  184.3 166.9 %collective-permute-start.2 = (bf16[256,4096]{1,0:T(8,128)(2,1)}, bf16[256,4096]{1,0:T(8,128)(2,1)}, u32[]{:S(2)}, u32[]{:S(2)}) collective-permute-start(bf16[256,4096]{1,0:T(8,128)(2,1)} %get-tuple-element.84), channel_id=1, source_target_pairs={{0,8},{8,16},{16,24},{24,0},{1,9},{9,17},{17,25},{25,1},{2,10},{10... | collective-permute-start | bytes 6291464 | tf_op jit(solution)/shard_map/ppermute | solution.py:256
  184.4 166.8 %collective-permute-start.3 = (bf16[256,4096]{1,0:T(8,128)(2,1)}, bf16[256,4096]{1,0:T(8,128)(2,1)}, u32[]{:S(2)}, u32[]{:S(2)}) collective-permute-start(bf16[256,4096]{1,0:T(8,128)(2,1)} %get-tuple-element.84), channel_id=1, source_target_pairs={{0,24},{8,0},{16,8},{24,16},{1,25},{9,1},{17,9},{25,17},{2,26},{10... | collective-permute-start | bytes 6291464 | tf_op jit(solution)/shard_map/ppermute | solution.py:256
  187.0 132.9 %collective-permute-start.8 = (bf16[256,4096]{1,0:T(8,128)(2,1)}, bf16[256,4096]{1,0:T(8,128)(2,1)}, u32[]{:S(2)}, u32[]{:S(2)}) collective-permute-start(bf16[256,4096]{1,0:T(8,128)(2,1)} %collective-permute-done.1.refs_1_), channel_id=1, source_target_pairs={{0,24},{8,0},{16,8},{24,16},{1,25},{9,1},{17,9},{25,17},{2,26},{10... | collective-permute-start | bytes 6291464 | tf_op jit(solution)/shard_map/ppermute | solution.py:274
  232.1 157.9 %collective-permute-start.16 = (bf16[256,4096]{1,0:T(8,128)(2,1)}, bf16[256,4096]{1,0:T(8,128)(2,1)}, u32[]{:S(2)}, u32[]{:S(2)}) collective-permute-start(bf16[256,4096]{1,0:T(8,128)(2,1)} %get-tuple-element.117), channel_id=1, source_target_pairs={{0,8},{8,16},{16,24},{24,0},{1,9},{9,17},{17,25},{25,1},{2,10},{10... | collective-permute-start | bytes 6291464 | tf_op jit(solution)/shard_map/ppermute | solution.py:256
  232.2 157.8 %collective-permute-start.17 = (bf16[256,4096]{1,0:T(8,128)(2,1)}, bf16[256,4096]{1,0:T(8,128)(2,1)}, u32[]{:S(2)}, u32[]{:S(2)}) collective-permute-start(bf16[256,4096]{1,0:T(8,128)(2,1)} %get-tuple-element.117), channel_id=1, source_target_pairs={{0,24},{8,0},{16,8},{24,16},{1,25},{9,1},{17,9},{25,17},{2,26},{10... | collective-permute-start | bytes 6291464 | tf_op jit(solution)/shard_map/ppermute | solution.py:256
  319.9 44.7 %collective-permute-start.13 = (bf16[256,4096]{1,0:T(8,128)(2,1)}, bf16[256,4096]{1,0:T(8,128)(2,1)}, u32[]{:S(2)}, u32[]{:S(2)}) collective-permute-start(bf16[256,4096]{1,0:T(8,128)(2,1)} %collective-permute-done.9.refs_3_), channel_id=1, source_target_pairs={{0,8},{8,16},{16,24},{24,0},{1,9},{9,17},{17,25},{25,1},{2,10},{10... | collective-permute-start | bytes 6291464 | tf_op jit(solution)/shard_map/ppermute | solution.py:272
  351.2 44.4 %collective-permute-start.15 = (bf16[256,4096]{1,0:T(8,128)(2,1)}, bf16[256,4096]{1,0:T(8,128)(2,1)}, u32[]{:S(2)}, u32[]{:S(2)}) collective-permute-start(bf16[256,4096]{1,0:T(8,128)(2,1)} %collective-permute-done.3.refs_1_), channel_id=1, source_target_pairs={{0,24},{8,0},{16,8},{24,16},{1,25},{9,1},{17,9},{25,17},{2,26},{10... | collective-permute-start | bytes 6291464 | tf_op jit(solution)/shard_map/ppermute | solution.py:274
  416.6 114.1 %reduce-scatter.10.cloned.1.call-start = ((), (), s32[]{:S(2)}) async-start(), calls=%async_computation.7 | async-start | bytes 4718592 | tf_op jit(solution)/shard_map/reduce_scatter | solution.py:322
  417.3 127.4 %reduce-scatter.12.cloned.1.call-start = ((), (), s32[]{:S(2)}) async-start(), calls=%async_computation.8 | async-start | bytes 7077888 | tf_op jit(solution)/shard_map/reduce_scatter | solution.py:322
  417.9 168.8 %reduce-scatter.14.cloned.1.call-start = ((), (), s32[]{:S(2)}) async-start(), calls=%async_computation.9 | async-start | bytes 7077888 | tf_op jit(solution)/shard_map/reduce_scatter | solution.py:322
  418.7 228.2 %reduce-scatter.6.cloned.1.call-start = ((), (), s32[]{:S(2)}) async-start(), calls=%async_computation.5 | async-start | bytes 4718592 | tf_op jit(solution)/shard_map/reduce_scatter | solution.py:341
  418.8 46.9 %collective-permute-start.11 = (bf16[256,4096]{1,0:T(8,128)(2,1)S(1)}, bf16[256,4096]{1,0:T(8,128)(2,1)S(1)}, u32[]{:S(2)}, u32[]{:S(2)}) collective-permute-start(bf16[256,4096]{1,0:T(8,128)(2,1)S(1)} %get-tuple-element.108), channel_id=1, source_target_pairs={{0,8},{8,16},{16,24},{24,0},{1,9},{9,17},{17,25},{25,1},{2,10},{10... | collective-permute-start | bytes 6291464 | tf_op jit(solution)/shard_map/ppermute | solution.py:256
  420.6 47.1 %collective-permute-start.12 = (bf16[256,4096]{1,0:T(8,128)(2,1)S(1)}, bf16[256,4096]{1,0:T(8,128)(2,1)}, u32[]{:S(2)}, u32[]{:S(2)}) collective-permute-start(bf16[256,4096]{1,0:T(8,128)(2,1)S(1)} %get-tuple-element.108), channel_id=1, source_target_pairs={{0,24},{8,0},{16,8},{24,16},{1,25},{9,1},{17,9},{25,17},{2,26},{10... | collective-permute-start | bytes 6291464 | tf_op jit(solution)/shard_map/ppermute | solution.py:256
  465.7 2.0 copy-start.5
  467.7 47.2 %collective-permute-start.19 = (bf16[256,4096]{1,0:T(8,128)(2,1)}, bf16[256,4096]{1,0:T(8,128)(2,1)S(1)}, u32[]{:S(2)}, u32[]{:S(2)}) collective-permute-start(bf16[256,4096]{1,0:T(8,128)(2,1)} %collective-permute-done.12.refs_0_), channel_id=1, source_target_pairs={{0,24},{8,0},{16,8},{24,16},{1,25},{9,1},{17,9},{25,17},{2,26},{10... | collective-permute-start | bytes 6291464 | tf_op jit(solution)/shard_map/ppermute | solution.py:274
  468.9 48.7 %collective-permute-start.20 = (bf16[256,4096]{1,0:T(8,128)(2,1)}, bf16[256,4096]{1,0:T(8,128)(2,1)}, u32[]{:S(2)}, u32[]{:S(2)}) collective-permute-start(bf16[256,4096]{1,0:T(8,128)(2,1)} %collective-permute-done.16.refs_3_), channel_id=1, source_target_pairs={{0,8},{8,16},{16,24},{24,0},{1,9},{9,17},{17,25},{25,1},{2,10},{10... | collective-permute-start | bytes 6291464 | tf_op jit(solution)/shard_map/ppermute | solution.py:272
  514.9 2.8 copy-start
  587.9 59.1 %collective-permute-start.23 = (bf16[256,768]{1,0:T(8,128)(2,1)S(1)}, bf16[256,768]{1,0:T(8,128)(2,1)S(1)}, u32[]{:S(2)}, u32[]{:S(2)}) collective-permute-start(bf16[256,768]{1,0:T(8,128)(2,1)S(1)} %pad_maximum_fusion), channel_id=1, source_target_pairs={{0,0},{1,4},{2,8},{3,12},{4,16},{5,20},{6,24},{7,28},{8,9},{9,13},... | collective-permute-start | bytes 1179656 | tf_op jit(solution)/shard_map/ppermute | solution.py:290
  591.6 55.4 %collective-permute-start.24 = (bf16[256,768]{1,0:T(8,128)(2,1)S(1)}, bf16[256,768]{1,0:T(8,128)(2,1)S(1)}, u32[]{:S(2)}, u32[]{:S(2)}) collective-permute-start(bf16[256,768]{1,0:T(8,128)(2,1)S(1)} %pad_maximum_fusion.1), channel_id=1, source_target_pairs={{0,4},{1,0},{2,12},{3,8},{4,20},{5,16},{6,28},{7,24},{8,13},{9,9},... | collective-permute-start | bytes 1179656 | tf_op jit(solution)/shard_map/ppermute | solution.py:290
  593.6 36.8 %collective-permute-start.22 = (bf16[256,512]{1,0:T(8,128)(2,1)S(1)}, bf16[256,512]{1,0:T(8,128)(2,1)S(1)}, u32[]{:S(2)}, u32[]{:S(2)}) collective-permute-start(bf16[256,512]{1,0:T(8,128)(2,1)S(1)} %pad_maximum_fusion.3), channel_id=1, source_target_pairs={{0,4},{1,0},{2,12},{3,8},{4,20},{5,16},{6,28},{7,24},{8,13},{9,9},... | collective-permute-start | bytes 786440 | tf_op jit(solution)/shard_map/ppermute | solution.py:290
  601.1 29.4 %collective-permute-start.21 = (bf16[256,512]{1,0:T(8,128)(2,1)S(1)}, bf16[256,512]{1,0:T(8,128)(2,1)S(1)}, u32[]{:S(2)}, u32[]{:S(2)}) collective-permute-start(bf16[256,512]{1,0:T(8,128)(2,1)S(1)} %pad_maximum_fusion.2), channel_id=1, source_target_pairs={{0,0},{1,4},{2,8},{3,12},{4,16},{5,20},{6,24},{7,28},{8,9},{9,13},... | collective-permute-start | bytes 786440 | tf_op jit(solution)/shard_map/ppermute | solution.py:290
  648.1 8.6 %collective-permute-start.25 = (bf16[256,256]{1,0:T(8,128)(2,1)S(1)}, bf16[256,256]{1,0:T(8,128)(2,1)S(1)}, u32[]{:S(2)}, u32[]{:S(2)}) collective-permute-start(bf16[256,256]{1,0:T(8,128)(2,1)S(1)} %get-tuple-element.178), channel_id=1, source_target_pairs={{0,4},{1,0},{2,12},{3,8},{4,20},{5,16},{6,28},{7,24},{8,13},{9,9},... | collective-permute-start | bytes 393224 | tf_op jit(solution)/shard_map/ppermute | solution.py:290
  653.6 8.4 %collective-permute-start.26 = (bf16[256,256]{1,0:T(8,128)(2,1)S(1)}, bf16[256,256]{1,0:T(8,128)(2,1)S(1)}, u32[]{:S(2)}, u32[]{:S(2)}) collective-permute-start(bf16[256,256]{1,0:T(8,128)(2,1)S(1)} %get-tuple-element.177), channel_id=1, source_target_pairs={{0,0},{1,4},{2,8},{3,12},{4,16},{5,20},{6,24},{7,28},{8,9},{9,13},... | collective-permute-start | bytes 393224 | tf_op jit(solution)/shard_map/ppermute | solution.py:290
Sparse Core Ops, SparseCore 0:
  26.4 42.1 all-gather.6
  70.3 28.5 all-gather.8
  182.8 24.1 all-gather.10
  416.8 47.2 reduce-scatter.7
  466.3 34.8 reduce-scatter.9
  503.4 41.3 reduce-scatter.11
  547.0 39.6 reduce-scatter.13
  589.0 57.9 reduce-scatter.5
